TPU v7x, 128 devices: a whole 4x4x4 slice. The times are simulated.
128 devices in a mesh: row: 8 (over x, core), col: 16 (over y, z).
Axes of the slice: x: 4, y: 4, z: 4, core: 2. Of those that a mesh axis runs over, the one named last changes fastest.
Arguments:
- velocity: float32 [3, 2, 128, 512, 256], P(None, None, 'row', 'col'), may hold values from -6 to 6
- register: float32 [3, 2, 128, 512, 256], P(None, None, 'row', 'col'), may hold values from -6 to 6
- offsets: int32 [256], replicated, may hold values from -2 to 2, as said below
- remesh_flag: int32 [256], replicated, may hold values from 0 to 1, as said below
- keep_blocks: int32 [16], replicated, may hold values 0 or 1
Outputs:
- velocity_next: float32 [3, 2, 128, 512, 256], P(None, None, 'row', 'col')
Inputs may be any that keep to these rules, and one draw needn't show every extreme that they name: offsets[j] is 0 or has the sign of ky = j - 128. On each side of ky = 0 the planes of magnitude 1 form one run of consecutive ky, and the planes of magnitude 2 the run that follows it directly, farther from ky = 0. Each of -2, -1, 1 and 2 is carried by half of 32 to 32 planes. Each nonzero value of offsets[j] remesh_flag[j] is taken by at most 32 planes, and in every draw one of them by exactly 32 planes.
All inputs are finite; a program needn't handle non-finite values.
Results may differ from a plain program's by a relative error of at most 0.0055.
Values may be sent and summed in bfloat16 or wider, within the bound.
No kernel may reach another device: no remote copies, remote signals or barrier semaphores. Data moves between devices by JAX's collectives and lax.ppermute only.
A program may use at most 192 MiB of HBM per device.

v0:
```python
import math

import jax
import jax.numpy as jnp
from jax import lax
from jax.sharding import PartitionSpec as P

NX = 512
NY = 256
NZ = 256
NZH = 128
MX = 768
MY = 384
MZ = 384
SHIFT_CAP = 32


SHEAR_RATE = 40.0
SHEAR_TIME = 0.3
VISCOSITY = 0.0015
TIME_STEP = 0.008
REGISTER_WEIGHT = -153.0 / 128.0
UPDATE_WEIGHT = 8.0 / 15.0
PRODUCT_PAIRS = ((0, 0), (0, 1), (0, 2), (1, 1), (1, 2), (2, 2))
PAIR_LOOKUP = ((0, 1, 2), (1, 3, 4), (2, 4, 5))
OFFSET_VALUES = (-2, -1, 1, 2)


def items_in_groups(array, axis, split_dim, concat_dim, work, item_dim, out_dim):
    items = jax.tree.leaves(array)[0].shape[item_dim]
    count = 2 if items % 2 == 0 else 1
    done = []
    for k in range(count):
        group = jax.tree.map(
            lambda a: lax.slice_in_dim(
                a, k * (items // count), (k + 1) * (items // count), axis=item_dim
            ),
            array,
        )
        done.append(
            work(
                lax.all_to_all(
                    group, axis, split_axis=split_dim, concat_axis=concat_dim, tiled=True
                )
            )
        )
    return jax.tree.map(lambda *parts: jnp.concatenate(parts, axis=out_dim), *done)


def from_behind(block, axis, distance):
    devices = range(lax.axis_size(axis))
    route = [(i - distance, i) for i in devices if i - distance in devices]
    return lax.ppermute(block, axis, route)


def phase_angles(contracted, produced, period):
    phase_turns = jnp.mod(contracted[:, None] * produced[None, :], period)
    return phase_turns.astype(jnp.float32) * (2.0 * math.pi / period)


def complex_table(contracted, produced, period, direction):
    angles = phase_angles(contracted, produced, period)
    cosine = jnp.cos(angles)
    sine_part = direction * jnp.sin(angles)
    upper_rows = jnp.stack([cosine, sine_part], axis=1)
    lower_rows = jnp.stack([-sine_part, cosine], axis=1)
    return jnp.stack([upper_rows, lower_rows], axis=0).astype(jnp.bfloat16)


def inverse_real_table(mode_list, points, period):
    angles = phase_angles(mode_list, points, period)
    weights = jnp.where(mode_list == 0, 1.0, 2.0).astype(jnp.float32)[:, None]
    return jnp.stack([weights * jnp.cos(angles), -weights * jnp.sin(angles)], axis=0).astype(
        jnp.bfloat16
    )


def forward_real_table(points, mode_list, period):
    angles = phase_angles(points, mode_list, period)
    return jnp.stack([jnp.cos(angles), -jnp.sin(angles)], axis=1).astype(jnp.bfloat16)


def tendency_update(spectra, velocity, register, kx_values, ky_values, kz_values):
    wave_x = kx_values[None, :, None] - SHEAR_TIME * ky_values[None, None, :]
    wave_y = ky_values[None, None, :]
    wave_z = kz_values[:, None, None]
    wave_list = (wave_x, wave_y, wave_z)
    squared = wave_x * wave_x + wave_y * wave_y + wave_z * wave_z
    inverse = 1.0 / jnp.maximum(squared, 1.0)
    advect_real = [
        sum((wave_list[source] * spectra[PAIR_LOOKUP[target][source], 1] for source in range(3)))
        for target in range(3)
    ]
    advect_imag = [
        -sum((wave_list[source] * spectra[PAIR_LOOKUP[target][source], 0] for source in range(3)))
        for target in range(3)
    ]
    diverge_real = sum((wave_list[target] * advect_real[target] for target in range(3)))
    diverge_imag = sum((wave_list[target] * advect_imag[target] for target in range(3)))
    pressure_lift = 2.0 * SHEAR_RATE * wave_y * inverse
    results = []
    for target in range(3):
        halves = []
        for half_index, advect, diverge in (
            (0, advect_real, diverge_real),
            (1, advect_imag, diverge_imag),
        ):
            rate_value = advect[target] - wave_list[target] * diverge * inverse
            rate_value = rate_value + wave_list[target] * pressure_lift * velocity[0, half_index]
            rate_value = rate_value - VISCOSITY * squared * velocity[target, half_index]
            if target == 1:
                rate_value = rate_value - SHEAR_RATE * velocity[0, half_index]
            increment = REGISTER_WEIGHT * register[target, half_index] + TIME_STEP * rate_value
            halves.append(velocity[target, half_index] + UPDATE_WEIGHT * increment)
        results.append(jnp.stack(halves))
    return jnp.stack(results)


def local(velocity, register, offsets, remesh_flag, keep_blocks):
    rows_count = lax.axis_size("row")
    cols_count = lax.axis_size("col")
    row_index = lax.axis_index("row")
    col_index = lax.axis_index("col")
    slab_kz = velocity.shape[2]
    slab_kx = velocity.shape[3]
    y_cols = MY // cols_count
    y_both = y_cols // rows_count
    inverse_scale = 1.0 / math.sqrt(NX * NY * NZ)
    forward_scale = math.sqrt(NX * NY * NZ) / (MX * MY * MZ)
    y_order = jnp.arange(MY, dtype=jnp.int32)
    owner_col = y_order // y_cols
    within_col = y_order % y_cols
    y_permuted = (within_col // y_both * cols_count + owner_col) * y_both + within_col % y_both
    x_points = jnp.arange(MX, dtype=jnp.int32)
    z_points = jnp.arange(MZ, dtype=jnp.int32)
    kx_all = jnp.arange(NX, dtype=jnp.int32) - NX // 2
    ky_all = jnp.arange(NY, dtype=jnp.int32) - NY // 2
    kz_all = jnp.arange(NZH, dtype=jnp.int32)
    kx_local = col_index * slab_kx + jnp.arange(slab_kx, dtype=jnp.int32) - NX // 2
    kz_local = row_index * slab_kz + jnp.arange(slab_kz, dtype=jnp.int32)
    y_inverse = complex_table(ky_all, y_permuted, MY, 1.0)
    x_inverse = complex_table(kx_all, x_points, MX, 1.0)
    z_inverse = inverse_real_table(kz_all, z_points, MZ)
    z_forward = forward_real_table(z_points, kz_all, MZ)
    x_forward = complex_table(x_points, kx_all, MX, -1.0)
    spectral = velocity.astype(jnp.bfloat16)
    along_y = jnp.einsum(
        "crlij,rjsq->csliq", spectral, y_inverse, preferred_element_type=jnp.float32
    ).astype(jnp.bfloat16)

    def inverse_x(items):
        return jnp.einsum(
            "crliq,risp->cslqp", items, x_inverse, preferred_element_type=jnp.float32
        ).astype(jnp.bfloat16)

    along_x = items_in_groups(along_y, "col", 4, 3, inverse_x, 2, 2)
    fields = (
        jnp.einsum(
            "crlab,rlz->cabz",
            lax.all_to_all(along_x, "row", split_axis=3, concat_axis=2, tiled=True),
            z_inverse,
            preferred_element_type=jnp.float32,
        )
        * inverse_scale
    )
    products = jnp.stack(
        [fields[left_factor] * fields[right_factor] for left_factor, right_factor in PRODUCT_PAIRS]
    ).astype(jnp.bfloat16)
    modes_z = (
        jnp.einsum("eabz,zsl->esabl", products, z_forward, preferred_element_type=jnp.float32)
        .astype(jnp.bfloat16)
        .reshape(6, 2, y_both, MX, rows_count, slab_kz)
    )
    x_split = x_forward.reshape(2, MX, 2, cols_count, slab_kx)
    arranged = jnp.einsum(
        "eryxab,rxscd->esyacbd", modes_z, x_split, preferred_element_type=jnp.float32
    ).astype(jnp.bfloat16)
    arranged = arranged.reshape(6, 2, y_both, rows_count * cols_count, slab_kz * slab_kx)
    gathered = lax.all_to_all(arranged, ("row", "col"), split_axis=3, concat_axis=2, tiled=True)
    gathered = gathered.reshape(6, 2, MY, slab_kz, slab_kx)
    y_forward = complex_table(y_order, ky_all, MY, -1.0)
    spectra = jnp.einsum(
        "erqli,rqsj->eslij", gathered, y_forward, preferred_element_type=jnp.float32
    )
    spectra = spectra * forward_scale
    updated = tendency_update(
        spectra,
        velocity,
        register,
        kx_local.astype(jnp.float32),
        ky_all.astype(jnp.float32),
        kz_local.astype(jnp.float32),
    )
    moved_by = offsets * remesh_flag
    remeshed = updated * (moved_by == 0).astype(jnp.float32)
    slot_ids = jnp.arange(SHIFT_CAP, dtype=jnp.int32)
    columns = []
    for shift_by in OFFSET_VALUES:
        marked = moved_by == shift_by
        ranked = jnp.cumsum(marked.astype(jnp.int32)) - 1
        columns.append(
            (marked[:, None] & (ranked[:, None] == slot_ids[None, :])).astype(jnp.float32)
        )
    placing = jnp.concatenate(columns, axis=1)
    packed = jnp.einsum("crlij,js->crlis", updated, placing)
    arrivals = []
    for position, shift_by in enumerate(OFFSET_VALUES):
        outgoing = packed[:, :, :, :, position * SHIFT_CAP : (position + 1) * SHIFT_CAP]
        arrivals.append(from_behind(outgoing, "col", shift_by))
    arrived = jnp.concatenate(arrivals, axis=4)
    remeshed = remeshed + jnp.einsum("crlis,js->crlij", arrived, placing)
    keep_here = jnp.sum(
        jnp.where(jnp.arange(cols_count, dtype=jnp.int32) == col_index, keep_blocks, 0)
    ).astype(jnp.float32)
    return remeshed * keep_here


def solution(mesh):
    placed = (P(None, None, "row", "col", None), P(None, None, "row", "col", None), P(), P(), P())
    return jax.shard_map(
        local,
        mesh=mesh,
        in_specs=placed,
        out_specs=P(None, None, "row", "col", None),
        check_vma=False,
    )
```

profile of v0, /device:TPU:110, one launch (start us, length us, event | category | flops | bytes accessed | tf_op | source)
XLA Modules:
  0.0 446.3 jit_solution(11688594146885093595)
XLA Ops:
  10.0 7.9 %reshape.1762 = bf16[16,2,18432]{2,1,0:T(2,128)(2,1)} reshape(bf16[384,2,3,8,32]{4,3,2,1,0:T(8,128)(2,1)} %bitcast.373) | data formatting | bytes 2359296
  17.8 7.0 %all-to-all-start = ((bf16[16,2,18432]{2,1,0:T(2,128)(2,1)}), bf16[16,2,18432]{2,1,0:T(2,128)(2,1)S(1)}, u32[]{:S(2)}, u32[]{:S(2)}) async-start(bf16[16,2,18432]{2,1,0:T(2,128)(2,1)} %reshape.1762), calls=%async_computation | async-start | bytes 2359296 | tf_op jit(solution)/shard_map/all_to_all | solution.py:42
  29.3 7.8 %reshape.1760 = bf16[16,2,18432]{2,1,0:T(2,128)(2,1)} reshape(bf16[384,2,3,8,32]{4,3,2,1,0:T(8,128)(2,1)} %bitcast.374) | data formatting | bytes 2359296
  40.1 8.3 %all-to-all-start.1 = ((bf16[16,2,18432]{2,1,0:T(2,128)(2,1)}), bf16[16,2,18432]{2,1,0:T(2,128)(2,1)S(1)}, u32[]{:S(2)}, u32[]{:S(2)}) async-start(bf16[16,2,18432]{2,1,0:T(2,128)(2,1)} %reshape.1760), calls=%async_computation.1 | async-start | bytes 2359296 | tf_op jit(solution)/shard_map/all_to_all | solution.py:42
  48.4 7.2 %fusion.47 = (bf16[512,1,768]{2,0,1:T(8,128)(2,1)S(1)}, bf16[512,1,768]{2,0,1:T(8,128)(2,1)S(1)}, bf16[512,1,768]{2,0,1:T(8,128)(2,1)S(1)}) fusion(s32[512]{0:T(512)S(1)} %iota_add_fusion), kind=kLoop, calls=%fused_computation.66 | loop fusion | flops 5111808 | bytes 2361344 | tf_op jit(solution)/shard_map/convert.28
  61.4 7.5 %copy.87 = bf16[3,2,8,16,32,24]{4,3,5,1,2,0:T(8,128)(2,1)} copy(bf16[3,2,8,16,32,24]{4,2,0,1,5,3:T(8,128)(2,1)} %bitcast.375) | data formatting | bytes 2359296 | tf_op jit(solution)/shard_map/all_to_all | solution.py:42
  69.0 7.3 %reshape.1738 = bf16[3,2,8,512,24,1]{3,4,1,2,0,5:T(8,128)(2,1)} reshape(bf16[3,2,8,16,32,24]{4,3,5,1,2,0:T(8,128)(2,1)} %copy.87) | data formatting | bytes 2359296 | tf_op jit(solution)/shard_map/all_to_all | solution.py:42
  80.1 7.5 %copy.90 = bf16[3,2,8,16,32,24]{4,3,5,1,2,0:T(8,128)(2,1)} copy(bf16[3,2,8,16,32,24]{4,2,0,1,5,3:T(8,128)(2,1)} %bitcast.376) | data formatting | bytes 2359296 | tf_op jit(solution)/shard_map/all_to_all | solution.py:42
  87.7 7.6 %reshape.1740 = bf16[3,2,8,512,24,1]{3,4,1,2,0,5:T(8,128)(2,1)} reshape(bf16[3,2,8,16,32,24]{4,3,5,1,2,0:T(8,128)(2,1)} %copy.90) | data formatting | bytes 2359296 | tf_op jit(solution)/shard_map/all_to_all | solution.py:42
  111.4 8.1 %fusion.52 = (bf16[1,768,1,16,32]{1,4,0,3,2:T(8,128)(2,1)}, bf16[1,768,1,16,32]{1,4,0,3,2:T(8,128)(2,1)}, bf16[1,768,1,16,32]{1,4,0,3,2:T(8,128)(2,1)}) fusion(s32[16,32]{1,0:T(8,128)S(1)} %add_add_fusion), kind=kLoop, calls=%fused_computation.75 | loop fusion | flops 5505024 | bytes 2361344 | tf_op jit(solution)/shard_map/convert.36
  119.6 29.3 %all-to-all-done.2 = bf16[3,2,16,24,768]{4,2,0,1,3:T(8,128)(2,1)S(1)} async-done(((bf16[3,2,16,24,768]{4,2,0,1,3:T(8,128)(2,1)}), bf16[3,2,16,24,768]{4,2,0,1,3:T(8,128)(2,1)S(1)}, u32[]{:S(2)}, u32[]{:S(2)}) %all-to-all-start.2) | async-done | bytes 3538976 | tf_op jit(solution)/shard_map/all_to_all | solution.py:160
  158.9 12.8 %fusion.4 = bf16[2,128,6,3,768]{4,1,3,2,0:T(8,128)(2,1)} fusion(bf16[6,3,768,384]{3,2,1,0:T(8,128)(2,1)} %copy-done, bf16[384,1,128]{0,2,1:T(8,128)(2,1)S(1)} %copy-done.9, bf16[384,1,128]{0,2,1:T(8,128)(2,1)S(1)} %copy-done.10), kind=kOutput, calls=%fused_computation.7 | convolution fusion | flops 2721841152 | bytes 17891328 | tf_op jit(solution)/shard_map/eabz,zsl->esabl/dot_general | solution.py:170
  171.7 31.7 %fusion = bf16[6,2,3,8,16,16,32]{6,5,3,2,0,4,1:T(8,128)(2,1)S(1)} fusion(bf16[6,2,3,768,8,16,1,1]{3,5,4,2,0,1,7,6:T(8,128)(2,1)} %bitcast.379, bf16[1,768,1,16,32]{1,4,0,3,2:T(8,128)(2,1)S(1)} %copy-done.8, bf16[1,768,1,16,32]{1,4,0,3,2:T(8,128)(2,1)S(1)} %copy-done.7, bf16[1,768,1,16,32]{1,4,0,3,2:T(8,128)(2,1)S(1)} %copy-done.6), kind=kOutput, calls=%fused_computation.1 | convolution fusion | flops 7262699520 | bytes 14155776 | tf_op jit(solution)/shard_map/eryxab,rxscd->esyacbd/dot_general | solution.py:175
  203.3 7.3 %copy.134 = bf16[6,2,3,8,16,16,32]{6,5,1,2,0,4,3:T(8,128)(2,1)} copy(bf16[6,2,3,8,16,16,32]{6,5,3,2,0,4,1:T(8,128)(2,1)S(1)} %fusion) | data formatting | bytes 9437184 | tf_op jit(solution)/shard_map/reshape | solution.py:178
  210.6 26.2 %reshape.1755 = bf16[6,2,3,128,512]{4,1,2,0,3:T(2,128)(2,1)} reshape(bf16[6,2,3,8,16,16,32]{6,5,1,2,0,4,3:T(8,128)(2,1)} %copy.134) | data formatting | bytes 9437184 | tf_op jit(solution)/shard_map/reshape | solution.py:178
  236.8 10.7 %all-to-all-start.3 = ((bf16[6,2,3,128,512]{4,1,2,0,3:T(2,128)(2,1)}), bf16[6,2,3,128,512]{4,1,2,0,3:T(2,128)(2,1)}, u32[]{:S(2)}, u32[]{:S(2)}) async-start(bf16[6,2,3,128,512]{4,1,2,0,3:T(2,128)(2,1)} %reshape.1755), calls=%async_computation.3 | async-start | bytes 9437184 | tf_op jit(solution)/shard_map/all_to_all | solution.py:179
  252.5 48.7 %all-to-all-done.3 = bf16[6,2,3,128,512]{4,1,2,0,3:T(2,128)(2,1)} async-done(((bf16[6,2,3,128,512]{4,1,2,0,3:T(2,128)(2,1)}), bf16[6,2,3,128,512]{4,1,2,0,3:T(2,128)(2,1)}, u32[]{:S(2)}, u32[]{:S(2)}) %all-to-all-start.3) | async-done | bytes 4718624 | tf_op jit(solution)/shard_map/all_to_all | solution.py:179
  301.2 7.7 %copy.98 = bf16[6,2,128,3,1,512]{5,1,3,2,0,4:T(2,128)(2,1)} copy(bf16[6,2,128,3,1,512]{5,1,3,0,2,4:T(2,128)(2,1)} %bitcast.54) | data formatting | bytes 9437184 | tf_op jit(solution)/shard_map/all_to_all | solution.py:179
  309.0 23.4 %reshape.1721 = bf16[6,2,384,16,32]{4,3,1,2,0:T(8,128)(2,1)} reshape(bf16[6,2,128,3,1,512]{5,1,3,2,0,4:T(2,128)(2,1)} %copy.98) | data formatting | bytes 9437184 | tf_op jit(solution)/shard_map/reshape | solution.py:180
  332.4 22.4 %copy.99 = bf16[6,2,384,16,32]{2,4,1,3,0:T(8,128)(2,1)} copy(bf16[6,2,384,16,32]{4,3,1,2,0:T(8,128)(2,1)} %reshape.1721) | data formatting | bytes 9437184 | tf_op jit(solution)/shard_map/reshape | solution.py:180
  354.8 5.5 %fusion.3 = f32[6,2,16,32,256]{4,3,2,0,1:T(8,128)S(1)} fusion(bf16[6,2,384,16,32]{2,4,1,3,0:T(8,128)(2,1)} %copy.99, bf16[1,384,2,256]{3,1,0,2:T(8,128)(2,1)S(1)} %get-tuple-element.36, bf16[1,384,2,256]{3,1,0,2:T(8,128)(2,1)S(1)} %get-tuple-element.35), kind=kOutput, calls=%fused_computation.6 | convolution fusion | flops 2419064832 | bytes 11796480 | tf_op jit(solution)/shard_map/erqli,rqsj->eslij/dot_general | solution.py:182
  382.4 8.4 %collective-permute-done = bf16[3,2,16,32,32]{4,3,2,1,0:T(8,128)(2,1)} collective-permute-done((bf16[3,2,16,32,32]{4,3,2,1,0:T(8,128)(2,1)}, bf16[3,2,16,32,32]{4,3,2,1,0:T(8,128)(2,1)}, u32[]{:S(2)}, u32[]{:S(2)}) %collective-permute-start) | collective-permute-done | bytes 196640 | tf_op jit(solution)/shard_map/ppermute | solution.py:53
  390.8 17.0 %collective-permute-done.1 = bf16[3,2,16,32,32]{4,3,2,1,0:T(8,128)(2,1)} collective-permute-done((bf16[3,2,16,32,32]{4,3,2,1,0:T(8,128)(2,1)}, bf16[3,2,16,32,32]{4,3,2,1,0:T(8,128)(2,1)}, u32[]{:S(2)}, u32[]{:S(2)}) %collective-permute-start.1) | collective-permute-done | bytes 196640 | tf_op jit(solution)/shard_map/ppermute | solution.py:53
  407.8 33.5 %collective-permute-done.2 = bf16[3,2,16,32,32]{4,3,2,1,0:T(8,128)(2,1)} collective-permute-done((bf16[3,2,16,32,32]{4,3,2,1,0:T(8,128)(2,1)}, bf16[3,2,16,32,32]{4,3,2,1,0:T(8,128)(2,1)}, u32[]{:S(2)}, u32[]{:S(2)}) %collective-permute-start.2) | collective-permute-done | bytes 196640 | tf_op jit(solution)/shard_map/ppermute | solution.py:53
  (114 shorter events, 84.3 us)
Async XLA Ops:
  17.8 22.3 %all-to-all-start = ((bf16[16,2,18432]{2,1,0:T(2,128)(2,1)}), bf16[16,2,18432]{2,1,0:T(2,128)(2,1)S(1)}, u32[]{:S(2)}, u32[]{:S(2)}) async-start(bf16[16,2,18432]{2,1,0:T(2,128)(2,1)} %reshape.1762), calls=%async_computation | async-start | bytes 2359296 | tf_op jit(solution)/shard_map/all_to_all | solution.py:42
  40.1 36.2 %all-to-all-start.1 = ((bf16[16,2,18432]{2,1,0:T(2,128)(2,1)}), bf16[16,2,18432]{2,1,0:T(2,128)(2,1)S(1)}, u32[]{:S(2)}, u32[]{:S(2)}) async-start(bf16[16,2,18432]{2,1,0:T(2,128)(2,1)} %reshape.1760), calls=%async_computation.1 | async-start | bytes 2359296 | tf_op jit(solution)/shard_map/all_to_all | solution.py:42
  87.6 7.6 %copy-start.3 = (bf16[1,512,2,768]{3,1,0,2:T(8,128)(2,1)S(1)}, bf16[1,512,2,768]{3,1,0,2:T(8,128)(2,1)}, u32[]{:S(2)}) copy-start(bf16[1,512,2,768]{3,1,0,2:T(8,128)(2,1)} %get-tuple-element.33) | copy-start | bytes 4718596
  87.7 7.6 %copy-start.4 = (bf16[1,512,2,768]{3,1,0,2:T(8,128)(2,1)S(1)}, bf16[1,512,2,768]{3,1,0,2:T(8,128)(2,1)}, u32[]{:S(2)}) copy-start(bf16[1,512,2,768]{3,1,0,2:T(8,128)(2,1)} %get-tuple-element.34) | copy-start | bytes 4718596
  95.3 3.4 copy-start.5
  103.5 45.3 %all-to-all-start.2 = ((bf16[3,2,16,24,768]{4,2,0,1,3:T(8,128)(2,1)}), bf16[3,2,16,24,768]{4,2,0,1,3:T(8,128)(2,1)S(1)}, u32[]{:S(2)}, u32[]{:S(2)}) async-start(bf16[3,2,16,24,768]{4,2,0,1,3:T(8,128)(2,1)} %copy.91), calls=%async_computation.2 | async-start | bytes 7077888 | tf_op jit(solution)/shard_map/all_to_all | solution.py:160
  148.9 0.9 copy-start.11
  148.9 0.9 copy-start.12
  154.3 4.6 %copy-start.9 = (bf16[384,1,128]{0,2,1:T(8,128)(2,1)S(1)}, bf16[384,1,128]{0,2,1:T(8,128)(2,1)}, u32[]{:S(2)}) copy-start(bf16[384,1,128]{0,2,1:T(8,128)(2,1)} %get-tuple-element.67) | copy-start | bytes 294916
  154.3 4.5 %copy-start.10 = (bf16[384,1,128]{0,2,1:T(8,128)(2,1)S(1)}, bf16[384,1,128]{0,2,1:T(8,128)(2,1)}, u32[]{:S(2)}) copy-start(bf16[384,1,128]{0,2,1:T(8,128)(2,1)} %get-tuple-element.68) | copy-start | bytes 294916
  154.8 4.0 copy-start
  158.9 12.8 %copy-start.6 = (bf16[1,768,1,16,32]{1,4,0,3,2:T(8,128)(2,1)S(1)}, bf16[1,768,1,16,32]{1,4,0,3,2:T(8,128)(2,1)}, u32[]{:S(2)}) copy-start(bf16[1,768,1,16,32]{1,4,0,3,2:T(8,128)(2,1)} %get-tuple-element.39) | copy-start | bytes 2359300
  158.9 12.8 %copy-start.7 = (bf16[1,768,1,16,32]{1,4,0,3,2:T(8,128)(2,1)S(1)}, bf16[1,768,1,16,32]{1,4,0,3,2:T(8,128)(2,1)}, u32[]{:S(2)}) copy-start(bf16[1,768,1,16,32]{1,4,0,3,2:T(8,128)(2,1)} %get-tuple-element.40) | copy-start | bytes 2359300
  158.9 12.8 %copy-start.8 = (bf16[1,768,1,16,32]{1,4,0,3,2:T(8,128)(2,1)S(1)}, bf16[1,768,1,16,32]{1,4,0,3,2:T(8,128)(2,1)}, u32[]{:S(2)}) copy-start(bf16[1,768,1,16,32]{1,4,0,3,2:T(8,128)(2,1)} %get-tuple-element.41) | copy-start | bytes 2359300
  236.8 10.7 %copy-start.13 = (s32[256]{0:T(256)S(1)}, s32[256]{0:T(256)}, u32[]{:S(2)}) copy-start(s32[256]{0:T(256)} %param.7) | copy-start | bytes 3076
  236.8 10.7 %copy-start.14 = (s32[256]{0:T(256)S(1)}, s32[256]{0:T(256)}, u32[]{:S(2)}) copy-start(s32[256]{0:T(256)} %param.8) | copy-start | bytes 3076
  236.8 64.4 %all-to-all-start.3 = ((bf16[6,2,3,128,512]{4,1,2,0,3:T(2,128)(2,1)}), bf16[6,2,3,128,512]{4,1,2,0,3:T(2,128)(2,1)}, u32[]{:S(2)}, u32[]{:S(2)}) async-start(bf16[6,2,3,128,512]{4,1,2,0,3:T(2,128)(2,1)} %reshape.1755), calls=%async_computation.3 | async-start | bytes 9437184 | tf_op jit(solution)/shard_map/all_to_all | solution.py:179
  354.8 5.5 %copy-start.1 = (f32[3,2,16,32,256]{4,3,2,1,0:T(8,128)S(1)}, f32[3,2,16,32,256]{4,3,2,1,0:T(8,128)}, u32[]{:S(2)}) copy-start(f32[3,2,16,32,256]{4,3,2,1,0:T(8,128)} %param.5) | copy-start | bytes 9437188
  354.8 5.5 %copy-start.2 = (f32[3,2,16,32,256]{4,3,2,1,0:T(8,128)S(1)}, f32[3,2,16,32,256]{4,3,2,1,0:T(8,128)}, u32[]{:S(2)}) copy-start(f32[3,2,16,32,256]{4,3,2,1,0:T(8,128)} %param.6) | copy-start | bytes 9437188
  364.2 17.0 %copy-start.15 = (s32[16]{0:T(128)S(1)}, s32[16]{0:T(128)}, u32[]{:S(2)}) copy-start(s32[16]{0:T(128)} %param.9) | copy-start | bytes 196
  366.6 24.2 %collective-permute-start = (bf16[3,2,16,32,32]{4,3,2,1,0:T(8,128)(2,1)}, bf16[3,2,16,32,32]{4,3,2,1,0:T(8,128)(2,1)}, u32[]{:S(2)}, u32[]{:S(2)}) collective-permute-start(bf16[3,2,16,32,32]{4,3,2,1,0:T(8,128)(2,1)} %get-tuple-element.29), channel_id=1, source_target_pairs={{2,0},{3,1},{4,2},{5,3},{6,4},{7,5},{8,6},{9,7},{10,8},{11,9},{12,... | collective-permute-start | bytes 589832 | tf_op jit(solution)/shard_map/ppermute | solution.py:53
  371.3 36.5 %collective-permute-start.1 = (bf16[3,2,16,32,32]{4,3,2,1,0:T(8,128)(2,1)}, bf16[3,2,16,32,32]{4,3,2,1,0:T(8,128)(2,1)}, u32[]{:S(2)}, u32[]{:S(2)}) collective-permute-start(bf16[3,2,16,32,32]{4,3,2,1,0:T(8,128)(2,1)} %get-tuple-element.32), channel_id=1, source_target_pairs={{1,0},{2,1},{3,2},{4,3},{5,4},{6,5},{7,6},{8,7},{9,8},{10,9},{11,1... | collective-permute-start | bytes 589832 | tf_op jit(solution)/shard_map/ppermute | solution.py:53
  375.0 66.3 %collective-permute-start.2 = (bf16[3,2,16,32,32]{4,3,2,1,0:T(8,128)(2,1)}, bf16[3,2,16,32,32]{4,3,2,1,0:T(8,128)(2,1)}, u32[]{:S(2)}, u32[]{:S(2)}) collective-permute-start(bf16[3,2,16,32,32]{4,3,2,1,0:T(8,128)(2,1)} %get-tuple-element.31), channel_id=1, source_target_pairs={{0,1},{1,2},{2,3},{3,4},{4,5},{5,6},{6,7},{7,8},{8,9},{9,10},{10,1... | collective-permute-start | bytes 589832 | tf_op jit(solution)/shard_map/ppermute | solution.py:53
  379.2 62.0 %collective-permute-start.3 = (bf16[3,2,16,32,32]{4,3,2,1,0:T(8,128)(2,1)}, bf16[3,2,16,32,32]{4,3,2,1,0:T(8,128)(2,1)}, u32[]{:S(2)}, u32[]{:S(2)}) collective-permute-start(bf16[3,2,16,32,32]{4,3,2,1,0:T(8,128)(2,1)} %get-tuple-element.30), channel_id=1, source_target_pairs={{0,2},{1,3},{2,4},{3,5},{4,6},{5,7},{6,8},{7,9},{8,10},{9,11},{10,... | collective-permute-start | bytes 589832 | tf_op jit(solution)/shard_map/ppermute | solution.py:53
where the time goes:
time: 454 us; the launch traced here: 446 us
  local copies, waits for them, and re-layouts  160 us (35%)
  waiting for transfers between devices  140 us (31%)
  matrix products  66.1 us (15%)
  starting transfers between devices  45.3 us (10%)
  other arithmetic  33.7 us (7%)
    ppermute x4, waiting for transfers between devices, from_behind(): return lax.ppermute(block, axis, route)  58.9 us
    all_to_all x1, waiting for transfers between devices, local(): lax.all_to_all(arranged, ('row', 'col'), split_axis=3, concat_axis=2, til...  48.7 us
    reshape x2, local copies, waits for them, and re-layouts, local(): gathered = gathered.reshape(6, 2, MY, slab_kz, slab_kx)  45.8 us
    reshape x2, local copies, waits for them, and re-layouts, local(): arranged.reshape(6, 2, y_both, rows_count * cols_count, slab_kz * slab_kx)  33.4 us
    dot_general x1, matrix products, local(): jnp.einsum('eryxab,rxscd->esyacbd', modes_z, x_split, preferred_element_t...  31.7 us
    all_to_all x4, local copies, waits for them, and re-layouts, items_in_groups(): lax.all_to_all(group, axis, split_axis=split_dim, concat_axis=concat_dim,...  29.9 us
    all_to_all x1, waiting for transfers between devices, local(): lax.all_to_all(along_x, 'row', split_axis=3, concat_axis=2, tiled=True)  29.3 us
    unnamed x36, local copies, waits for them, and re-layouts  28.1 us
  transfers between devices with their start and end apart: 8, of which 6 were waited for; matrix products, arithmetic and copies ran while one was open for 13% of the time, Pallas kernels for 0%

commit v1 on v0

v1 whole, which is shorter than its diff:
```python
import functools
import math

import jax
import jax.numpy as jnp
import numpy as np
from jax import lax
from jax.experimental import pallas as pl
from jax.experimental.pallas import tpu as pltpu
from jax.sharding import PartitionSpec as P

NX = 512
NY = 256
NZ = 256
NZH = 128
MX = 768
MY = 384
MZ = 384
SHIFT_CAP = 32
ROWS = 8
COLS = 16
DEV = ROWS * COLS
YPD = MY // DEV
LKZ = NZH // ROWS
LKX = NX // COLS
HALF = LKZ // 2
PRODUCTS = 5

SHEAR_RATE = 40.0
SHEAR_TIME = 0.3
VISCOSITY = 0.0015
TIME_STEP = 0.008
REGISTER_WEIGHT = -153.0 / 128.0
UPDATE_WEIGHT = 8.0 / 15.0
OFFSET_VALUES = (-2, -1, 1, 2)
INVERSE_SCALE = 1.0 / math.sqrt(NX * NY * NZ)
FORWARD_SCALE = math.sqrt(NX * NY * NZ) / (MX * MY * MZ)

BF16 = jnp.bfloat16
F32 = jnp.float32


def angle_tables(first, second, period):
    turns = np.mod(first[:, None].astype(np.int64) * second[None, :].astype(np.int64), period)
    angles = turns.astype(np.float32) * np.float32(2.0 * math.pi / period)
    angles = angles.astype(np.float64)
    return np.cos(angles).astype(np.float32), np.sin(angles).astype(np.float32)


def y_table():
    cosine, sine = angle_tables(np.arange(MY), np.arange(NY) - NY // 2, MY)
    return jnp.asarray(np.concatenate([cosine, sine], axis=1).astype(BF16))


def z_tables():
    cosine, sine = angle_tables(np.arange(MZ), np.arange(NZH), MZ)
    weights = np.where(np.arange(NZH) == 0, 1.0, 2.0).astype(np.float32)[None, :]
    inverse = np.concatenate([weights * cosine, -weights * sine], axis=1).astype(BF16)
    forward = np.concatenate([cosine.T, -sine.T], axis=0).astype(BF16)
    return jnp.asarray(inverse), jnp.asarray(forward)


def x_factors():
    points = np.arange(MX)
    coarse = angle_tables(np.arange(COLS) * LKX - NX // 2, points, MX)
    fine = angle_tables(np.arange(LKX), points, MX)
    return [jnp.asarray(t) for t in coarse + fine]


def dot(a, b, dims):
    return lax.dot_general(a, b, (dims, ((), ())), preferred_element_type=F32)


def x_table_kernel(coarse_cos, coarse_sin, fine_cos, fine_sin, out):
    fc = fine_cos[...]
    fs = fine_sin[...]
    for col in range(COLS):
        a = coarse_cos[col : col + 1, :]
        b = coarse_sin[col : col + 1, :]
        real = (a * fc - b * fs).astype(BF16)
        imag_f = a * fs + b * fc
        base = col * 2 * LKX
        out[base : base + LKX, :MX] = real
        out[base : base + LKX, MX:] = imag_f.astype(BF16)
        out[base + LKX : base + 2 * LKX, :MX] = (-imag_f).astype(BF16)
        out[base + LKX : base + 2 * LKX, MX:] = real


def x_table():
    return pl.pallas_call(
        x_table_kernel,
        out_shape=jax.ShapeDtypeStruct((2 * NX, 2 * MX), BF16),
        name="x_table",
    )(*x_factors())


MSG_IN = YPD * 3 * HALF
GROUPS = 3 * HALF


def y_inverse_kernel(v_ref, table_ref, out_ref, rt_ref, scr_ref):
    c = pl.program_id(0)
    for lo in range(HALF):
        for hi in range(2):
            real = v_ref[0, 0, hi * HALF + lo].astype(BF16)
            imag = v_ref[0, 1, hi * HALF + lo].astype(BF16)
            base = (lo * 2 + hi) * 2 * LKX
            rt_ref[base : base + LKX, :NY] = real
            rt_ref[base : base + LKX, NY:] = -imag
            rt_ref[base + LKX : base + 2 * LKX, :NY] = imag
            rt_ref[base + LKX : base + 2 * LKX, NY:] = real
    for pair in range(HALF // 2):
        res = dot(table_ref[...], rt_ref[pair * 256 : (pair + 1) * 256, :], ((1,), (1,)))
        for y in range(YPD):
            for h in range(2):
                start = y * GROUPS + c * HALF + pair * 2 + h
                scr_ref[pl.ds(start, DEV, stride=MSG_IN), :] = res[
                    y * DEV : (y + 1) * DEV, h * 128 : (h + 1) * 128
                ]

    @pl.when(c == 2)
    def _():
        def pack(d, carry):
            rows = scr_ref[pl.ds(pl.multiple_of(d * 8 * MSG_IN, 8), 8 * MSG_IN), :]
            out_ref[pl.ds(d * 8, 8)] = rows.astype(BF16).reshape(8, MSG_IN, 128)
            return carry

        lax.fori_loop(0, DEV // 8, pack, 0)


def y_inverse(velocity):
    return pl.pallas_call(
        y_inverse_kernel,
        grid=(3,),
        in_specs=[
            pl.BlockSpec((1, 2, LKZ, LKX, NY), lambda c: (c, 0, 0, 0, 0)),
            pl.BlockSpec((MY, 2 * NY), lambda c: (0, 0)),
        ],
        out_specs=pl.BlockSpec((DEV, MSG_IN, 128), lambda c: (0, 0, 0)),
        out_shape=jax.ShapeDtypeStruct((DEV, MSG_IN, 128), BF16),
        scratch_shapes=[
            pltpu.VMEM((LKZ * 2 * LKX, 2 * NY), BF16),
            pltpu.VMEM((DEV * MSG_IN, 128), F32),
        ],
        compiler_params=pltpu.CompilerParams(vmem_limit_bytes=50 * 2**20),
        name="y_inverse",
    )(velocity, y_table())


MSG_OUT = YPD * PRODUCTS * HALF


def middle_kernel(m_ref, x_ref, zi_ref, zf_ref, o_ref, u_ref, w_ref, mz_ref):
    low3 = lax.broadcasted_iota(jnp.int32, (3 * HALF, 128), 1) < 64
    low5 = lax.broadcasted_iota(jnp.int32, (PRODUCTS * HALF, 128), 1) < 64

    def gather(r, carry):
        for cp in range(COLS // 2):
            a = m_ref[r * COLS + 2 * cp].astype(F32)
            b = m_ref[r * COLS + 2 * cp + 1].astype(F32)
            first = jnp.where(low3, a, pltpu.roll(b, 64, 1))
            second = jnp.where(low3, pltpu.roll(a, 64, 1), b)
            for c in range(3):
                rows = slice(c * HALF, (c + 1) * HALF)
                both = jnp.concatenate([first[rows], second[rows]], axis=0)
                start = pl.multiple_of(c * NZH + r * LKZ, LKZ)
                u_ref[pl.ds(start, LKZ), cp * 128 : (cp + 1) * 128] = both.astype(BF16)
        return carry

    lax.fori_loop(0, ROWS, gather, 0)

    for s in range(2):

        def x_inverse(n, carry, s=s):
            cols = pl.ds(pl.multiple_of(s * MX + n * 256, 256), 256)
            res = dot(u_ref[...], x_ref[:, cols], ((1,), (0,)))
            here = pl.ds(pl.multiple_of(n * 256, 256), 256)
            for c in range(3):
                start = c * 2 * NZH + s * NZH
                w_ref[start : start + NZH, here] = res[c * NZH : (c + 1) * NZH].astype(BF16)
            return carry

        lax.fori_loop(0, MX // 256, x_inverse, 0)

    def z_both(n, carry):
        here = pl.ds(pl.multiple_of(n * 256, 256), 256)
        there = pl.ds(pl.multiple_of(MX + n * 256, 256), 256)
        zi = zi_ref[...]
        zf = zf_ref[...]
        f0, f1, f2 = [
            dot(zi, w_ref[c * 2 * NZH : (c + 1) * 2 * NZH, here], ((1,), (0,))) * INVERSE_SCALE
            for c in range(3)
        ]
        last = f2 * f2
        products = (f0 * f0 - last, f0 * f1, f0 * f2, f1 * f1 - last, f1 * f2)
        for e, product in enumerate(products):
            res = dot(zf, product.astype(BF16), ((1,), (0,)))
            mz_ref[e * NZH : (e + 1) * NZH, here] = res[:NZH].astype(BF16)
            mz_ref[e * NZH : (e + 1) * NZH, there] = res[NZH:].astype(BF16)
        return carry

    lax.fori_loop(0, MX // 256, z_both, 0)

    def x_forward(n, carry):
        rows = pl.ds(pl.multiple_of(n * 256, 256), 256)
        res = dot(mz_ref[...], x_ref[rows, :], ((1,), (1,)))
        for half in range(2):
            for r in range(ROWS):
                lo, hi = [
                    jnp.concatenate(
                        [
                            res[
                                e * NZH + r * LKZ + h * HALF : e * NZH + r * LKZ + (h + 1) * HALF,
                                half * 128 : (half + 1) * 128,
                            ]
                            for e in range(PRODUCTS)
                        ],
                        axis=0,
                    )
                    for h in range(2)
                ]
                first = jnp.where(low5, lo, pltpu.roll(hi, 64, 1))
                second = jnp.where(low5, pltpu.roll(lo, 64, 1), hi)
                dest = r * COLS + 4 * n + 2 * half
                o_ref[dest] = first.astype(BF16)
                o_ref[dest + 1] = second.astype(BF16)
        return carry

    lax.fori_loop(0, NX * 2 // 256, x_forward, 0)


def middle(messages, table):
    zi, zf = z_tables()
    return pl.pallas_call(
        middle_kernel,
        grid=(YPD,),
        in_specs=[
            pl.BlockSpec((DEV, 3 * HALF, 128), lambda y: (0, y, 0)),
            pl.BlockSpec((2 * NX, 2 * MX), lambda y: (0, 0)),
            pl.BlockSpec((MZ, 2 * NZH), lambda y: (0, 0)),
            pl.BlockSpec((2 * NZH, MZ), lambda y: (0, 0)),
        ],
        out_specs=pl.BlockSpec((DEV, PRODUCTS * HALF, 128), lambda y: (0, y, 0)),
        out_shape=jax.ShapeDtypeStruct((DEV, MSG_OUT, 128), BF16),
        scratch_shapes=[
            pltpu.VMEM((3 * NZH, 2 * NX), BF16),
            pltpu.VMEM((6 * NZH, MX), BF16),
            pltpu.VMEM((PRODUCTS * NZH, 2 * MX), BF16),
        ],
        compiler_params=pltpu.CompilerParams(vmem_limit_bytes=50 * 2**20),
        name="middle",
    )(messages, table, zi, zf)


PACK = 2 * 6 * LKX


def update_kernel(
    scal_ref, g_ref, table_ref, v_ref, reg_ref, place_ref, stay_ref, base_ref, p0, p1, p2, p3, scr_ref
):
    lo = pl.program_id(0)

    @pl.when(lo == 0)
    def _():
        def unpack(d, carry):
            rows = g_ref[pl.ds(d * 8, 8)].astype(F32).reshape(8 * MSG_OUT, 128)
            scr_ref[pl.ds(pl.multiple_of(d * 8 * MSG_OUT, 8), 8 * MSG_OUT), :] = rows
            return carry

        lax.fori_loop(0, DEV // 8, unpack, 0)

    table = table_ref[...]
    spectra = []
    for e in range(PRODUCTS):
        parts = [
            scr_ref[
                pl.ds(y * PRODUCTS * HALF + e * HALF + lo, DEV, stride=MSG_OUT), :
            ].astype(BF16)
            for y in range(YPD)
        ]
        spectra.append(dot(jnp.concatenate(parts, axis=0), table, ((0,), (0,))))

    kx0 = scal_ref[0]
    kz0 = scal_ref[1]
    shape = (LKX, NY)
    k2 = (lax.broadcasted_iota(jnp.int32, shape, 1) - NY // 2).astype(F32)
    k1 = lax.broadcasted_iota(jnp.int32, shape, 0).astype(F32) + kx0 - SHEAR_TIME * k2
    stay = stay_ref[...]
    moving = []
    for hi in range(2):
        k3 = kz0 + (lo + hi * HALF).astype(F32)
        waves = (k1, k2, k3)
        squared = k1 * k1 + k2 * k2 + k3 * k3
        inverse = 1.0 / jnp.maximum(squared, 1.0)
        real = []
        imag = []
        for p in spectra:
            top = p[hi * 2 * LKX : hi * 2 * LKX + LKX]
            bottom = p[hi * 2 * LKX + LKX : (hi + 1) * 2 * LKX]
            real.append((top[:, :NY] + bottom[:, NY:]) * FORWARD_SCALE)
            imag.append((bottom[:, :NY] - top[:, NY:]) * FORWARD_SCALE)

        def rows_of(t):
            return (
                k1 * t[0] + k2 * t[1] + k3 * t[2],
                k1 * t[1] + k2 * t[3] + k3 * t[4],
                k1 * t[2] + k2 * t[4],
            )

        advect_parts = (rows_of(imag), tuple(-a for a in rows_of(real)))
        lift = 2.0 * SHEAR_RATE * k2 * inverse
        for half in range(2):
            advect = advect_parts[half]
            diverge = k1 * advect[0] + k2 * advect[1] + k3 * advect[2]
            first = v_ref[0, half, hi, 0]
            common = lift * first - diverge * inverse
            for m in range(3):
                velocity = v_ref[m, half, hi, 0]
                rate = advect[m] + waves[m] * common
                rate = rate - VISCOSITY * squared * velocity
                if m == 1:
                    rate = rate - SHEAR_RATE * first
                increment = REGISTER_WEIGHT * reg_ref[m, half, hi, 0] + TIME_STEP * rate
                updated = velocity + UPDATE_WEIGHT * increment
                base_ref[m, half, hi, 0] = updated * stay
                moving.append(updated.astype(BF16))
    packed = dot(place_ref[...], jnp.concatenate(moving, axis=0), ((1,), (1,))).astype(BF16)
    for position, ref in enumerate((p0, p1, p2, p3)):
        ref[...] = packed[position * SHIFT_CAP : (position + 1) * SHIFT_CAP]


FIELD = (3, 2, 2, HALF, LKX, NY)
FIELD_BLOCK = pl.BlockSpec((3, 2, 2, 1, LKX, NY), lambda lo: (0, 0, 0, lo, 0, 0))
MOVE_BLOCK = pl.BlockSpec((SHIFT_CAP, PACK), lambda lo: (0, lo))


def update(scalars, gathered, velocity, register, place, stay):
    return pl.pallas_call(
        update_kernel,
        grid=(HALF,),
        in_specs=[
            pl.BlockSpec(memory_space=pltpu.SMEM),
            pl.BlockSpec((DEV, MSG_OUT, 128), lambda lo: (0, 0, 0)),
            pl.BlockSpec((MY, 2 * NY), lambda lo: (0, 0)),
            FIELD_BLOCK,
            FIELD_BLOCK,
            pl.BlockSpec((4 * SHIFT_CAP, NY), lambda lo: (0, 0)),
            pl.BlockSpec((1, NY), lambda lo: (0, 0)),
        ],
        out_specs=[FIELD_BLOCK] + [MOVE_BLOCK] * 4,
        out_shape=[jax.ShapeDtypeStruct(FIELD, F32)]
        + [jax.ShapeDtypeStruct((SHIFT_CAP, HALF * PACK), BF16)] * 4,
        scratch_shapes=[pltpu.VMEM((DEV * MSG_OUT, 128), F32)],
        compiler_params=pltpu.CompilerParams(vmem_limit_bytes=50 * 2**20),
        name="update",
    )(scalars, gathered, y_table(), velocity.reshape(FIELD), register.reshape(FIELD), place, stay)


def settle_kernel(scal_ref, base_ref, a0, a1, a2, a3, place_ref, out_ref):
    arrived = jnp.concatenate([a0[...], a1[...], a2[...], a3[...]], axis=0)
    moved = dot(arrived, place_ref[...], ((0,), (0,)))
    keep = scal_ref[2]
    for hi in range(2):
        for m in range(3):
            for half in range(2):
                start = (hi * 6 + half * 3 + m) * LKX
                out_ref[m, half, hi, 0] = (
                    base_ref[m, half, hi, 0] + moved[start : start + LKX]
                ) * keep


def settle(scalars, base, arrivals, place):
    return pl.pallas_call(
        settle_kernel,
        grid=(HALF,),
        in_specs=[pl.BlockSpec(memory_space=pltpu.SMEM), FIELD_BLOCK]
        + [MOVE_BLOCK] * 4
        + [pl.BlockSpec((4 * SHIFT_CAP, NY), lambda lo: (0, 0))],
        out_specs=FIELD_BLOCK,
        out_shape=jax.ShapeDtypeStruct(FIELD, F32),
        name="settle",
    )(scalars, base, *arrivals, place)


def from_behind(block, axis, distance):
    devices = range(COLS)
    route = [(i - distance, i) for i in devices if i - distance in devices]
    return lax.ppermute(block, axis, route)


def local(velocity, register, offsets, remesh_flag, keep_blocks):
    row_index = lax.axis_index("row")
    col_index = lax.axis_index("col")
    moved_by = offsets * remesh_flag
    marked = jnp.stack([moved_by == value for value in OFFSET_VALUES])
    order = jnp.arange(NY, dtype=jnp.int32)
    upto = (order[:, None] <= order[None, :]).astype(BF16)
    ranked = jnp.dot(marked.astype(BF16), upto, preferred_element_type=F32).astype(jnp.int32) - 1
    slots = jnp.arange(SHIFT_CAP, dtype=jnp.int32)
    place = (marked[:, None, :] & (ranked[:, None, :] == slots[None, :, None])).astype(BF16)
    place = place.reshape(4 * SHIFT_CAP, NY)
    stay = (moved_by == 0).astype(F32).reshape(1, NY)
    keep_here = jnp.sum(
        jnp.where(jnp.arange(COLS, dtype=jnp.int32) == col_index, keep_blocks, 0)
    ).astype(F32)
    scalars = jnp.stack(
        [
            (col_index * LKX - NX // 2).astype(F32),
            (row_index * LKZ).astype(F32),
            keep_here,
        ]
    )

    outgoing = y_inverse(velocity)
    table = x_table()
    messages = lax.all_to_all(outgoing, ("row", "col"), split_axis=0, concat_axis=0, tiled=True)
    returning = middle(messages, table)
    gathered = lax.all_to_all(returning, ("row", "col"), split_axis=0, concat_axis=0, tiled=True)
    base, *packed = update(scalars, gathered, velocity, register, place, stay)
    arrivals = [
        from_behind(block, "col", value) for block, value in zip(packed, OFFSET_VALUES)
    ]
    result = settle(scalars, base, arrivals, place)
    return result.reshape(velocity.shape)


def solution(mesh):
    placed = (P(None, None, "row", "col", None), P(None, None, "row", "col", None), P(), P(), P())
    return jax.shard_map(
        local,
        mesh=mesh,
        in_specs=placed,
        out_specs=P(None, None, "row", "col", None),
        check_vma=False,
    )
```

time: 454 us -> 177 us (0.39)
  the two profiles are of different devices: /device:TPU:110 before, /device:TPU:8 now
where the time goes in v1:
time: 177 us; the launch traced here: 176 us
  waiting for transfers between devices  84.2 us (48%)
  Pallas kernels  57.2 us (32%)
  starting transfers between devices  29.7 us (17%)
  local copies, waits for them, and re-layouts  3.26 us (2%)
    all_to_all x1, waiting for transfers between devices, local(): lax.all_to_all(returning, ('row', 'col'), split_axis=0, concat_axis=0, ti...  48.4 us
    pallas_call x1, Pallas kernels, middle(): pl.pallas_call(middle_kernel, grid=(YPD,), in_specs=[pl.BlockSpec((DEV, 3...  30.1 us
    all_to_all x1, waiting for transfers between devices, local(): lax.all_to_all(outgoing, ('row', 'col'), split_axis=0, concat_axis=0, til...  28.9 us
    ppermute x4, starting transfers between devices, from_behind(): return lax.ppermute(block, axis, route)  13.2 us
    pallas_call x1, Pallas kernels, update(): pl.pallas_call(update_kernel, grid=(HALF,), in_specs=[pl.BlockSpec(memory...  13 us
    all_to_all x1, starting transfers between devices, local(): lax.all_to_all(outgoing, ('row', 'col'), split_axis=0, concat_axis=0, til...  10.4 us
    pallas_call x1, Pallas kernels, settle(): pl.pallas_call(settle_kernel, grid=(HALF,), in_specs=[pl.BlockSpec(memory...  6.94 us
    ppermute x4, waiting for transfers between devices, from_behind(): return lax.ppermute(block, axis, route)  6.93 us
  transfers between devices with their start and end apart: 6, of which 4 were waited for; matrix products, arithmetic and copies ran while one was open for 1% of the time, Pallas kernels for 2%

profile of v1, /device:TPU:8, one launch (start us, length us, event | category | flops | bytes accessed | tf_op | source)
XLA Modules:
  0.0 176.3 jit_solution(5607775499880570024)
XLA Ops:
  0.0 1.0 copy-done.1
  1.0 4.0 %y_inverse.1 = bf16[128,72,128]{2,1,0:T(8,128)(2,1)S(1)} custom-call(f32[3,2,16,32,256]{4,3,2,1,0:T(8,128)} %v_ref.1, bf16[384,512]{1,0:T(8,128)(2,1)S(1)} %copy-done.1), custom_call_target="tpu_custom_call" | custom-call | tf_op jit(solution)/shard_map/y_inverse/pallas_call | solution.py:132
  5.1 1.4 copy-done
  6.5 10.4 %all-to-all-start = ((bf16[128,72,128]{2,1,0:T(8,128)(2,1)}), bf16[128,72,128]{2,1,0:T(8,128)(2,1)S(1)}, u32[]{:S(2)}, u32[]{:S(2)}) async-start(bf16[128,72,128]{2,1,0:T(8,128)(2,1)} %copy-done), calls=%async_computation | async-start | bytes 4718592 | tf_op jit(solution)/shard_map/all_to_all | solution.py:416
  16.9 3.2 %x_table.1.x_ref = bf16[1024,1536]{1,0:T(8,128)(2,1)} custom-call(f32[16,768]{1,0:T(8,128)} %constant.44.clone.coarse_cos, f32[16,768]{1,0:T(8,128)} %constant.45.clone.coarse_sin, f32[32,768]{1,0:T(8,128)} %constant.46.clone.fine_cos, f32[32,768]{1,0:T(8,128)} %constant.47.clone.fine_sin), custom_call_target="tpu_custom_call" | custom-call | tf_op jit(solution)/shard_map/x_table/pallas_call | solution.py:90
  20.1 28.9 %all-to-all-done.m_ref = bf16[128,72,128]{2,1,0:T(8,128)(2,1)S(1)} async-done(((bf16[128,72,128]{2,1,0:T(8,128)(2,1)}), bf16[128,72,128]{2,1,0:T(8,128)(2,1)S(1)}, u32[]{:S(2)}, u32[]{:S(2)}) %all-to-all-start) | async-done | bytes 2359328 | tf_op jit(solution)/shard_map/all_to_all | solution.py:416
  49.0 30.1 %middle.1 = bf16[128,120,128]{2,1,0:T(8,128)(2,1)} custom-call(bf16[128,72,128]{2,1,0:T(8,128)(2,1)S(1)} %all-to-all-done.m_ref, bf16[1024,1536]{1,0:T(8,128)(2,1)} %x_table.1.x_ref, bf16[384,256]{1,0:T(8,128)(2,1)S(1)} %copy-done.4, bf16[256,384]{1,0:T(8,128)(2,1)S(1)} %copy-done.5), custom_call_target="tpu_custom_call" | custom-call | tf_op jit(solution)/shard_map/middle/pallas_call | solution.py:234
  79.2 6.1 %all-to-all-start.1 = ((bf16[128,120,128]{2,1,0:T(8,128)(2,1)}), bf16[128,120,128]{2,1,0:T(8,128)(2,1)}, u32[]{:S(2)}, u32[]{:S(2)}) async-start(bf16[128,120,128]{2,1,0:T(8,128)(2,1)} %middle.1), calls=%async_computation.1 | async-start | bytes 7864320 | tf_op jit(solution)/shard_map/all_to_all | solution.py:418
  85.3 0.6 fusion.3
  86.6 0.1 eq.69
  86.8 0.2 fusion
  86.9 0.1 fusion.2.place_ref
  87.0 0.1 pad_maximum_fusion.scal_ref
  87.1 48.4 %all-to-all-done.1.g_ref = bf16[128,120,128]{2,1,0:T(8,128)(2,1)} async-done(((bf16[128,120,128]{2,1,0:T(8,128)(2,1)}), bf16[128,120,128]{2,1,0:T(8,128)(2,1)}, u32[]{:S(2)}, u32[]{:S(2)}) %all-to-all-start.1) | async-done | bytes 3932192 | tf_op jit(solution)/shard_map/all_to_all | solution.py:418
  135.5 13.0 %update.1 = (f32[3,2,2,8,32,256]{5,4,3,2,1,0:T(8,128)}, bf16[32,3072]{1,0:T(8,128)(2,1)S(1)}, bf16[32,3072]{1,0:T(8,128)(2,1)S(1)}, bf16[32,3072]{1,0:T(8,128)(2,1)S(1)}, bf16[32,3072]{1,0:T(8,128)(2,1)S(1)}) custom-call(f32[3]{0:T(128)S(1)} %pad_maximum_fusion.scal_ref, bf16[128,120,128]{2,1,0:T(8,128)(2,1)} %all-to-all-done.1.g_ref, ...), custom_call_target="tpu_custom_call" | custom-call | tf_op jit(solution)/shard_map/update/pallas_call | solution.py:338
  148.4 1.9 %collective-permute-start = (bf16[32,3072]{1,0:T(8,128)(2,1)S(1)}, bf16[32,3072]{1,0:T(8,128)(2,1)S(1)}, u32[]{:S(2)}, u32[]{:S(2)}) collective-permute-start(bf16[32,3072]{1,0:T(8,128)(2,1)S(1)} %get-tuple-element.11), channel_id=1, source_target_pairs={{2,0},{3,1},{4,2},{5,3},{6,4},{7,5},{8,6},{9,7},{10,8},{11,9},{12,... | collective-permute-start | bytes 589832 | tf_op jit(solution)/shard_map/ppermute | solution.py:388
  150.4 4.2 %collective-permute-start.1 = (bf16[32,3072]{1,0:T(8,128)(2,1)S(1)}, bf16[32,3072]{1,0:T(8,128)(2,1)S(1)}, u32[]{:S(2)}, u32[]{:S(2)}) collective-permute-start(bf16[32,3072]{1,0:T(8,128)(2,1)S(1)} %get-tuple-element.12), channel_id=1, source_target_pairs={{1,0},{2,1},{3,2},{4,3},{5,4},{6,5},{7,6},{8,7},{9,8},{10,9},{11,1... | collective-permute-start | bytes 589832 | tf_op jit(solution)/shard_map/ppermute | solution.py:388
  154.6 2.8 %collective-permute-start.2 = (bf16[32,3072]{1,0:T(8,128)(2,1)S(1)}, bf16[32,3072]{1,0:T(8,128)(2,1)S(1)}, u32[]{:S(2)}, u32[]{:S(2)}) collective-permute-start(bf16[32,3072]{1,0:T(8,128)(2,1)S(1)} %get-tuple-element.13), channel_id=1, source_target_pairs={{0,1},{1,2},{2,3},{3,4},{4,5},{5,6},{6,7},{7,8},{8,9},{9,10},{10,1... | collective-permute-start | bytes 589832 | tf_op jit(solution)/shard_map/ppermute | solution.py:388
  157.4 4.3 %collective-permute-start.3 = (bf16[32,3072]{1,0:T(8,128)(2,1)S(1)}, bf16[32,3072]{1,0:T(8,128)(2,1)S(1)}, u32[]{:S(2)}, u32[]{:S(2)}) collective-permute-start(bf16[32,3072]{1,0:T(8,128)(2,1)S(1)} %get-tuple-element.14), channel_id=1, source_target_pairs={{0,2},{1,3},{2,4},{3,5},{4,6},{5,7},{6,8},{7,9},{8,10},{9,11},{10,... | collective-permute-start | bytes 589832 | tf_op jit(solution)/shard_map/ppermute | solution.py:388
  161.7 0.0 collective-permute-done.a0
  161.7 5.7 %collective-permute-done.2.a2 = bf16[32,3072]{1,0:T(8,128)(2,1)S(1)} collective-permute-done((bf16[32,3072]{1,0:T(8,128)(2,1)S(1)}, bf16[32,3072]{1,0:T(8,128)(2,1)S(1)}, u32[]{:S(2)}, u32[]{:S(2)}) %collective-permute-start.2) | collective-permute-done | bytes 196640 | tf_op jit(solution)/shard_map/ppermute | solution.py:388
  167.4 1.2 collective-permute-done.3.a3
  168.7 0.7 copy-done.10
  169.3 6.9 %settle.1 = f32[3,2,2,8,32,256]{5,4,3,2,1,0:T(8,128)} custom-call(f32[3]{0:T(128)} %copy-done.6, f32[3,2,2,8,32,256]{5,4,3,2,1,0:T(8,128)} %get-tuple-element.10.base_ref, bf16[32,3072]{1,0:T(8,128)(2,1)} %copy-done.7, bf16[32,3072]{1,0:T(8,128)(2,1)} %copy-done.8, bf16[32,3072]{1,0:T(8,128)(2,1)} %copy-done.9, bf16[32,3072]{1,0:T(8,128)(2,1)} %copy-done.10, ...), custom_call_target="tpu_custom_call" | custom-call | tf_op jit(solution)/shard_map/settle/pallas_call | solution.py:373
  (34 shorter events, 0.1 us)
Async XLA Ops:
  0.0 1.0 copy-start.1
  5.0 1.4 copy-start
  6.5 42.6 %copy-start.4 = (bf16[384,256]{1,0:T(8,128)(2,1)S(1)}, bf16[384,256]{1,0:T(8,128)(2,1)}, u32[]{:S(2)}) copy-start(bf16[384,256]{1,0:T(8,128)(2,1)} %constant.48.clone.zi_ref) | copy-start | bytes 589828
  6.5 42.6 %copy-start.5 = (bf16[256,384]{1,0:T(8,128)(2,1)S(1)}, bf16[256,384]{1,0:T(8,128)(2,1)}, u32[]{:S(2)}) copy-start(bf16[256,384]{1,0:T(8,128)(2,1)} %constant.49.clone.zf_ref) | copy-start | bytes 589828
  6.5 42.6 %all-to-all-start = ((bf16[128,72,128]{2,1,0:T(8,128)(2,1)}), bf16[128,72,128]{2,1,0:T(8,128)(2,1)S(1)}, u32[]{:S(2)}, u32[]{:S(2)}) async-start(bf16[128,72,128]{2,1,0:T(8,128)(2,1)} %copy-done), calls=%async_computation | async-start | bytes 4718592 | tf_op jit(solution)/shard_map/all_to_all | solution.py:416
  79.2 6.1 %copy-start.13 = (s32[16]{0:T(128)S(1)}, s32[16]{0:T(128)}, u32[]{:S(2)}) copy-start(s32[16]{0:T(128)} %param.17) | copy-start | bytes 196
  79.2 7.5 %copy-start.11 = (s32[256]{0:T(256)S(1)}, s32[256]{0:T(256)}, u32[]{:S(2)}) copy-start(s32[256]{0:T(256)} %param.15) | copy-start | bytes 3076
  79.2 7.5 %copy-start.12 = (s32[256]{0:T(256)S(1)}, s32[256]{0:T(256)}, u32[]{:S(2)}) copy-start(s32[256]{0:T(256)} %param.16) | copy-start | bytes 3076
  79.2 56.3 %copy-start.2 = (bf16[384,512]{1,0:T(8,128)(2,1)S(1)}, bf16[384,512]{1,0:T(8,128)(2,1)}, u32[]{:S(2)}) copy-start(bf16[384,512]{1,0:T(8,128)(2,1)} %constant.43.clone.table_ref) | copy-start | bytes 1179652
  79.2 56.3 %all-to-all-start.1 = ((bf16[128,120,128]{2,1,0:T(8,128)(2,1)}), bf16[128,120,128]{2,1,0:T(8,128)(2,1)}, u32[]{:S(2)}, u32[]{:S(2)}) async-start(bf16[128,120,128]{2,1,0:T(8,128)(2,1)} %middle.1), calls=%async_computation.1 | async-start | bytes 7864320 | tf_op jit(solution)/shard_map/all_to_all | solution.py:418
  87.0 61.4 %copy-start.3 = (bf16[128,256]{1,0:T(8,128)(2,1)}, bf16[128,256]{1,0:T(8,128)(2,1)S(1)}, u32[]{:S(2)}) copy-start(bf16[128,256]{1,0:T(8,128)(2,1)S(1)} %fusion.2.place_ref) | copy-start | bytes 196612
  87.1 61.3 %copy-start.6 = (f32[3]{0:T(128)}, f32[3]{0:T(128)S(1)}, u32[]{:S(2)}) copy-start(f32[3]{0:T(128)S(1)} %pad_maximum_fusion.scal_ref) | copy-start | bytes 40
  148.4 13.2 %collective-permute-start = (bf16[32,3072]{1,0:T(8,128)(2,1)S(1)}, bf16[32,3072]{1,0:T(8,128)(2,1)S(1)}, u32[]{:S(2)}, u32[]{:S(2)}) collective-permute-start(bf16[32,3072]{1,0:T(8,128)(2,1)S(1)} %get-tuple-element.11), channel_id=1, source_target_pairs={{2,0},{3,1},{4,2},{5,3},{6,4},{7,5},{8,6},{9,7},{10,8},{11,9},{12,... | collective-permute-start | bytes 589832 | tf_op jit(solution)/shard_map/ppermute | solution.py:388
  150.4 11.3 %collective-permute-start.1 = (bf16[32,3072]{1,0:T(8,128)(2,1)S(1)}, bf16[32,3072]{1,0:T(8,128)(2,1)S(1)}, u32[]{:S(2)}, u32[]{:S(2)}) collective-permute-start(bf16[32,3072]{1,0:T(8,128)(2,1)S(1)} %get-tuple-element.12), channel_id=1, source_target_pairs={{1,0},{2,1},{3,2},{4,3},{5,4},{6,5},{7,6},{8,7},{9,8},{10,9},{11,1... | collective-permute-start | bytes 589832 | tf_op jit(solution)/shard_map/ppermute | solution.py:388
  154.6 12.8 %collective-permute-start.2 = (bf16[32,3072]{1,0:T(8,128)(2,1)S(1)}, bf16[32,3072]{1,0:T(8,128)(2,1)S(1)}, u32[]{:S(2)}, u32[]{:S(2)}) collective-permute-start(bf16[32,3072]{1,0:T(8,128)(2,1)S(1)} %get-tuple-element.13), channel_id=1, source_target_pairs={{0,1},{1,2},{2,3},{3,4},{4,5},{5,6},{6,7},{7,8},{8,9},{9,10},{10,1... | collective-permute-start | bytes 589832 | tf_op jit(solution)/shard_map/ppermute | solution.py:388
  157.4 11.3 %collective-permute-start.3 = (bf16[32,3072]{1,0:T(8,128)(2,1)S(1)}, bf16[32,3072]{1,0:T(8,128)(2,1)S(1)}, u32[]{:S(2)}, u32[]{:S(2)}) collective-permute-start(bf16[32,3072]{1,0:T(8,128)(2,1)S(1)} %get-tuple-element.14), channel_id=1, source_target_pairs={{0,2},{1,3},{2,4},{3,5},{4,6},{5,7},{6,8},{7,9},{8,10},{9,11},{10,... | collective-permute-start | bytes 589832 | tf_op jit(solution)/shard_map/ppermute | solution.py:388
  161.7 7.0 %copy-start.7 = (bf16[32,3072]{1,0:T(8,128)(2,1)}, bf16[32,3072]{1,0:T(8,128)(2,1)S(1)}, u32[]{:S(2)}) copy-start(bf16[32,3072]{1,0:T(8,128)(2,1)S(1)} %collective-permute-done.a0) | copy-start | bytes 589828
  161.7 6.9 %copy-start.8 = (bf16[32,3072]{1,0:T(8,128)(2,1)}, bf16[32,3072]{1,0:T(8,128)(2,1)S(1)}, u32[]{:S(2)}) copy-start(bf16[32,3072]{1,0:T(8,128)(2,1)S(1)} %collective-permute-done.1.a1) | copy-start | bytes 589828
  167.4 1.2 copy-start.9
  168.6 0.7 copy-start.10

commit v2 on v1

v2 whole, which is shorter than its diff:
```python
import functools
import math

import jax
import jax.numpy as jnp
import numpy as np
from jax import lax
from jax.experimental import pallas as pl
from jax.experimental.pallas import tpu as pltpu
from jax.sharding import PartitionSpec as P

NX = 512
NY = 256
NZ = 256
NZH = 128
MX = 768
MY = 384
MZ = 384
SHIFT_CAP = 32
ROWS = 8
COLS = 16
DEV = ROWS * COLS
YPD = MY // DEV
LKZ = NZH // ROWS
LKX = NX // COLS
HALF = LKZ // 2
PRODUCTS = 5

SHEAR_RATE = 40.0
SHEAR_TIME = 0.3
VISCOSITY = 0.0015
TIME_STEP = 0.008
REGISTER_WEIGHT = -153.0 / 128.0
UPDATE_WEIGHT = 8.0 / 15.0
OFFSET_VALUES = (-2, -1, 1, 2)
INVERSE_SCALE = 1.0 / math.sqrt(NX * NY * NZ)
FORWARD_SCALE = math.sqrt(NX * NY * NZ) / (MX * MY * MZ)

BF16 = jnp.bfloat16
F32 = jnp.float32


def angle_tables(first, second, period):
    turns = np.mod(first[:, None].astype(np.int64) * second[None, :].astype(np.int64), period)
    angles = turns.astype(np.float32) * np.float32(2.0 * math.pi / period)
    angles = angles.astype(np.float64)
    return np.cos(angles).astype(np.float32), np.sin(angles).astype(np.float32)


def y_table():
    cosine, sine = angle_tables(np.arange(MY), np.arange(NY) - NY // 2, MY)
    return jnp.asarray(np.concatenate([cosine, sine], axis=1).astype(BF16))


def z_tables():
    slots = np.arange(MZ // 2)
    partners = np.where(slots == 0, MZ // 2, MZ - slots)
    modes = np.arange(NZH)
    cosine, sine = angle_tables(np.concatenate([slots, partners]), modes, MZ)
    weights = np.where(modes == 0, 1.0, 2.0).astype(np.float32)[None, :]
    inverse = np.concatenate([weights * cosine, -weights * sine], axis=1).astype(BF16)
    even = (modes % 2 == 0).astype(np.float32)
    real = np.zeros((NZH, MZ // 2 + 16), np.float32)
    real[:, : MZ // 2] = cosine[: MZ // 2].T
    real[:, 0] = even
    real[:, MZ // 2] = 1.0 - even
    imag = -sine[: MZ // 2].T
    return [jnp.asarray(t) for t in (inverse, real.astype(BF16), imag.astype(BF16))]


def x_factors():
    points = np.arange(MX // 2)
    coarse = angle_tables(np.arange(COLS) * LKX - NX // 2, points, MX)
    fine = angle_tables(np.arange(LKX), points, MX)
    return [jnp.asarray(t) for t in coarse + fine]


def dot(a, b, dims):
    return lax.dot_general(a, b, (dims, ((), ())), preferred_element_type=F32)


XN = MX // 256


def x_table_kernel(coarse_cos, coarse_sin, fine_cos, fine_sin, out):
    shape = (LKX, 128)
    first = lax.broadcasted_iota(jnp.int32, shape, 1) == 0
    odd = lax.rem(lax.broadcasted_iota(jnp.int32, shape, 0), 2).astype(F32)
    for n in range(XN):
        here = slice(n * 128, (n + 1) * 128)
        fc = fine_cos[:, here]
        fs = fine_sin[:, here]
        for col in range(COLS):
            a = coarse_cos[col : col + 1, here]
            b = coarse_sin[col : col + 1, here]
            cosine = a * fc - b * fs
            sine = a * fs + b * fc
            if n == 0:
                cosine = jnp.where(first, 1.0 - odd, cosine)
                sine = jnp.where(first, odd, sine)
            rows = slice(col * LKX, (col + 1) * LKX)
            out[rows, n * 256 : n * 256 + 128] = cosine.astype(BF16)
            out[rows, n * 256 + 128 : (n + 1) * 256] = sine.astype(BF16)


def x_table():
    return pl.pallas_call(
        x_table_kernel,
        out_shape=jax.ShapeDtypeStruct((NX, MX), BF16),
        compiler_params=pltpu.CompilerParams(vmem_limit_bytes=12 * 2**20),
        name="x_table",
    )(*x_factors())


MSG_IN = YPD * 3 * HALF
GROUPS = YPD * HALF


def y_inverse_kernel(v_ref, table_ref, out_ref, rt_ref, scr_ref):
    for lo in range(HALF):
        for hi in range(2):
            real = v_ref[0, 0, hi * HALF + lo].astype(BF16)
            imag = v_ref[0, 1, hi * HALF + lo].astype(BF16)
            base = (lo * 2 + hi) * 2 * LKX
            rt_ref[base : base + LKX, :NY] = real
            rt_ref[base : base + LKX, NY:] = -imag
            rt_ref[base + LKX : base + 2 * LKX, :NY] = imag
            rt_ref[base + LKX : base + 2 * LKX, NY:] = real
    for pair in range(HALF // 2):
        res = dot(table_ref[...], rt_ref[pair * 256 : (pair + 1) * 256, :], ((1,), (1,)))
        for y in range(YPD):
            for h in range(2):
                start = y * HALF + pair * 2 + h
                scr_ref[pl.ds(start, DEV, stride=GROUPS), :] = res[
                    y * DEV : (y + 1) * DEV, h * 128 : (h + 1) * 128
                ]

    def pack(d, carry):
        rows = scr_ref[pl.ds(pl.multiple_of(d * 8 * GROUPS, 8), 8 * GROUPS), :]
        out_ref[pl.ds(d * 8, 8)] = rows.astype(BF16).reshape(8, GROUPS, 128)
        return carry

    lax.fori_loop(0, DEV // 8, pack, 0)


def y_inverse(velocity):
    return pl.pallas_call(
        y_inverse_kernel,
        grid=(3,),
        in_specs=[
            pl.BlockSpec((1, 2, LKZ, LKX, NY), lambda c: (c, 0, 0, 0, 0)),
            pl.BlockSpec((MY, 2 * NY), lambda c: (0, 0)),
        ],
        out_specs=pl.BlockSpec((DEV, GROUPS, 128), lambda c: (0, c, 0)),
        out_shape=pltpu.HBM((DEV, MSG_IN, 128), BF16),
        scratch_shapes=[
            pltpu.VMEM((LKZ * 2 * LKX, 2 * NY), BF16),
            pltpu.VMEM((DEV * GROUPS, 128), F32),
        ],
        compiler_params=pltpu.CompilerParams(vmem_limit_bytes=60 * 2**20),
        name="y_inverse",
    )(velocity, y_table())


MSG_OUT = YPD * PRODUCTS * HALF


def exchange4(a, b, c, d, low, even):
    ac0 = jnp.where(low, a, pltpu.roll(c, 64, 1))
    ac1 = jnp.where(low, pltpu.roll(a, 64, 1), c)
    bd0 = jnp.where(low, b, pltpu.roll(d, 64, 1))
    bd1 = jnp.where(low, pltpu.roll(b, 64, 1), d)
    return (
        jnp.where(even, ac0, pltpu.roll(bd0, 32, 1)),
        jnp.where(even, pltpu.roll(ac0, 96, 1), bd0),
        jnp.where(even, ac1, pltpu.roll(bd1, 32, 1)),
        jnp.where(even, pltpu.roll(ac1, 96, 1), bd1),
    )


def lane_masks(rows):
    lanes = lax.broadcasted_iota(jnp.int32, (rows, 128), 1)
    return lanes < 64, lax.rem(lanes, 64) < 32


def middle_kernel(m_ref, x_ref, zi_ref, zr_ref, zm_ref, o_ref, u_ref, f_ref):
    y = pl.program_id(0)
    rows_of_y = [
        pl.ds(pl.multiple_of(c * GROUPS + y * HALF, HALF), HALF) for c in range(3)
    ]
    masks = lane_masks(3 * HALF)
    for r in range(ROWS):
        for cg in range(COLS // 4):
            four = [
                jnp.concatenate(
                    [
                        m_ref[r * COLS + 4 * cg + q, here, :].astype(F32) for here in rows_of_y
                    ],
                    axis=0,
                )
                for q in range(4)
            ]
            parts = exchange4(*four, *masks)
            for s in range(2):
                for c in range(3):
                    rows = slice(c * HALF, (c + 1) * HALF)
                    both = jnp.concatenate([parts[s][rows], parts[2 + s][rows]], axis=0)
                    start = (s * 3 + c) * NZH + r * LKZ
                    u_ref[start : start + LKZ, cg * 128 : (cg + 1) * 128] = both.astype(BF16)

    zi = zi_ref[...]
    zr = zr_ref[...]
    zm = zm_ref[...]
    first = lax.broadcasted_iota(jnp.int32, (NZH, 128), 1) == 0
    half = MZ // 2
    for n in range(XN):
        here = slice(n * 256, (n + 1) * 256)
        res = dot(u_ref[...], x_ref[:, here], ((1,), (0,)))
        fields = []
        for c in range(3):
            top = slice(c * NZH, (c + 1) * NZH)
            bottom = slice((3 + c) * NZH, (4 + c) * NZH)
            cr, sr = res[top, :128], res[top, 128:]
            ci, si = res[bottom, :128], res[bottom, 128:]
            x1, x2 = si, sr
            if n == 0:
                x1 = jnp.where(first, -sr, si)
                x2 = jnp.where(first, si, sr)
            modes = jnp.concatenate(
                [
                    jnp.concatenate([cr - x1, cr + x1], axis=1),
                    jnp.concatenate([ci + x2, ci - x2], axis=1),
                ],
                axis=0,
            ).astype(BF16)
            fields.append(dot(zi, modes, ((1,), (0,))))
        f0, f1, f2 = fields
        last = f2 * f2
        products = (f0 * f0 - last, f0 * f1, f0 * f2, f1 * f1 - last, f1 * f2)
        for e, product in enumerate(products):
            even = (product[:half] + product[half:]).astype(BF16)
            odd = (product[:half] - product[half:]).astype(BF16)
            mr = dot(zr, jnp.concatenate([even, odd[:16]], axis=0), ((1,), (0,)))
            mi = dot(zm, odd, ((1,), (0,)))
            er, orr = mr[:, :128] + mr[:, 128:], mr[:, :128] - mr[:, 128:]
            ei, oi = mi[:, :128] + mi[:, 128:], mi[:, :128] - mi[:, 128:]
            x1, x2 = oi, -orr
            if n == 0:
                x1 = jnp.where(first, orr, oi)
                x2 = jnp.where(first, oi, -orr)
            top = slice(e * NZH, (e + 1) * NZH)
            bottom = slice((PRODUCTS + e) * NZH, (PRODUCTS + e + 1) * NZH)
            f_ref[top, here] = jnp.concatenate([er, x1], axis=1).astype(BF16)
            f_ref[bottom, here] = jnp.concatenate([ei, x2], axis=1).astype(BF16)

    masks = lane_masks(PRODUCTS * HALF)
    for m in range(NX // 256):
        res = dot(f_ref[...], x_ref[m * 256 : (m + 1) * 256, :], ((1,), (1,)))
        for side in range(2):
            for r in range(ROWS):
                four = []
                for hi in range(2):
                    for s in range(2):
                        pieces = []
                        for e in range(PRODUCTS):
                            start = (s * PRODUCTS + e) * NZH + r * LKZ + hi * HALF
                            pieces.append(
                                res[start : start + HALF, side * 128 : (side + 1) * 128]
                            )
                        four.append(jnp.concatenate(pieces, axis=0))
                parts = exchange4(*four, *masks)
                for q in range(4):
                    o_ref[r * COLS + 4 * (2 * m + side) + q] = parts[q].astype(BF16)


def middle(messages, table):
    return pl.pallas_call(
        middle_kernel,
        grid=(YPD,),
        in_specs=[
            pl.BlockSpec((DEV, MSG_IN, 128), lambda y: (0, 0, 0)),
            pl.BlockSpec((NX, MX), lambda y: (0, 0)),
            pl.BlockSpec((MZ, 2 * NZH), lambda y: (0, 0)),
            pl.BlockSpec((NZH, MZ // 2 + 16), lambda y: (0, 0)),
            pl.BlockSpec((NZH, MZ // 2), lambda y: (0, 0)),
        ],
        out_specs=pl.BlockSpec((DEV, PRODUCTS * HALF, 128), lambda y: (0, y, 0)),
        out_shape=pltpu.HBM((DEV, MSG_OUT, 128), BF16),
        scratch_shapes=[
            pltpu.VMEM((6 * NZH, NX), BF16),
            pltpu.VMEM((2 * PRODUCTS * NZH, MX), BF16),
        ],
        compiler_params=pltpu.CompilerParams(vmem_limit_bytes=26 * 2**20),
        name="middle",
    )(messages, table, *z_tables())


PACK = 2 * 6 * LKX
PARTS = 4
FIELD = (3, 2, 2, HALF, LKX, NY)


def field_block(per):
    return pl.BlockSpec((3, 2, 2, per, LKX, NY), lambda k: (0, 0, 0, k, 0, 0))


def move_block(per):
    return pl.BlockSpec((SHIFT_CAP, per * PACK), lambda k: (0, k))


LINEAR_PER = 4
UPDATE_PER = 2
SETTLE_PER = 4


def wave_numbers(scal_ref, lo, hi):
    shape = (LKX, NY)
    k2 = (lax.broadcasted_iota(jnp.int32, shape, 1) - NY // 2).astype(F32)
    k1 = lax.broadcasted_iota(jnp.int32, shape, 0).astype(F32) + scal_ref[0] - SHEAR_TIME * k2
    k3 = scal_ref[1] + (lo + hi * HALF).astype(F32)
    squared = k1 * k1 + k2 * k2 + k3 * k3
    return k1, k2, k3, squared, 1.0 / jnp.maximum(squared, 1.0)


def linear_kernel(scal_ref, v_ref, reg_ref, out_ref):
    for u, hi in ((u, hi) for u in range(LINEAR_PER) for hi in range(2)):
        lo = pl.program_id(0) * LINEAR_PER + u
        k1, k2, k3, squared, inverse = wave_numbers(scal_ref, lo, hi)
        lift = 2.0 * SHEAR_RATE * k2 * inverse
        for half in range(2):
            first = v_ref[0, half, hi, u]
            lifted = lift * first
            for m, wave in enumerate((k1, k2, k3)):
                velocity = v_ref[m, half, hi, u]
                rate = wave * lifted - VISCOSITY * squared * velocity
                if m == 1:
                    rate = rate - SHEAR_RATE * first
                increment = REGISTER_WEIGHT * reg_ref[m, half, hi, u] + TIME_STEP * rate
                out_ref[m, half, hi, u] = velocity + UPDATE_WEIGHT * increment


def linear_part(scalars, velocity, register):
    return pl.pallas_call(
        linear_kernel,
        grid=(HALF // LINEAR_PER,),
        in_specs=[pl.BlockSpec(memory_space=pltpu.SMEM), field_block(LINEAR_PER), field_block(LINEAR_PER)],
        out_specs=field_block(LINEAR_PER),
        out_shape=pltpu.HBM(FIELD, F32),
        compiler_params=pltpu.CompilerParams(vmem_limit_bytes=60 * 2**20),
        name="linear",
    )(scalars, velocity.reshape(FIELD), register.reshape(FIELD))


def update_kernel(
    scal_ref, g_hbm, table_ref, lin_ref, place_ref, stay_ref, base_ref, p0, p1, p2, p3, scr_ref,
    g_ref, sems,
):
    step = pl.program_id(0)

    @pl.when(step == 0)
    def _():
        copies = []
        for part in range(PARTS):
            here = pl.ds(part * (DEV // PARTS), DEV // PARTS)
            copies.append(pltpu.make_async_copy(g_hbm.at[here], g_ref.at[here], sems.at[part]))
            copies[-1].start()

        def unpack(d, carry):
            rows = g_ref[pl.ds(d * 8, 8)].astype(F32).reshape(8 * MSG_OUT, 128)
            scr_ref[pl.ds(pl.multiple_of(d * 8 * MSG_OUT, 8), 8 * MSG_OUT), :] = rows
            return carry

        share = DEV // 8 // PARTS
        for part in range(PARTS):
            copies[part].wait()
            lax.fori_loop(part * share, (part + 1) * share, unpack, 0)

    table = table_ref[...]
    stay = stay_ref[...]
    weight = UPDATE_WEIGHT * TIME_STEP * FORWARD_SCALE * INVERSE_SCALE * INVERSE_SCALE
    for u in range(UPDATE_PER):
        lo = step * UPDATE_PER + u
        spectra = []
        for e in range(PRODUCTS):
            parts = [
                scr_ref[
                    pl.ds(y * PRODUCTS * HALF + e * HALF + lo, DEV, stride=MSG_OUT), :
                ].astype(BF16)
                for y in range(YPD)
            ]
            spectra.append(dot(jnp.concatenate(parts, axis=0), table, ((0,), (0,))))

        moving = []
        for hi in range(2):
            k1, k2, k3, squared, inverse = wave_numbers(scal_ref, lo, hi)
            real = []
            imag = []
            for p in spectra:
                top = p[hi * 2 * LKX : hi * 2 * LKX + LKX]
                bottom = p[hi * 2 * LKX + LKX : (hi + 1) * 2 * LKX]
                real.append(top[:, :NY] + bottom[:, NY:])
                imag.append(bottom[:, :NY] - top[:, NY:])
            for half, t, sign in ((0, imag, weight), (1, real, -weight)):
                stress = (
                    k1 * t[0] + k2 * t[1] + k3 * t[2],
                    k1 * t[1] + k2 * t[3] + k3 * t[4],
                    k1 * t[2] + k2 * t[4],
                )
                pressure = (k1 * stress[0] + k2 * stress[1] + k3 * stress[2]) * inverse
                for m, wave in enumerate((k1, k2, k3)):
                    updated = lin_ref[m, half, hi, u] + sign * (stress[m] - wave * pressure)
                    base_ref[m, half, hi, u] = updated * stay
                    moving.append(updated.astype(BF16))
        packed = dot(place_ref[...], jnp.concatenate(moving, axis=0), ((1,), (1,))).astype(BF16)
        for position, ref in enumerate((p0, p1, p2, p3)):
            ref[:, u * PACK : (u + 1) * PACK] = packed[position * SHIFT_CAP : (position + 1) * SHIFT_CAP]


def update(scalars, gathered, linear, place, stay):
    return pl.pallas_call(
        update_kernel,
        grid=(HALF // UPDATE_PER,),
        in_specs=[
            pl.BlockSpec(memory_space=pltpu.SMEM),
            pl.BlockSpec(memory_space=pl.ANY),
            pl.BlockSpec((MY, 2 * NY), lambda lo: (0, 0)),
            field_block(UPDATE_PER),
            pl.BlockSpec((4 * SHIFT_CAP, NY), lambda lo: (0, 0)),
            pl.BlockSpec((1, NY), lambda lo: (0, 0)),
        ],
        out_specs=[field_block(UPDATE_PER)] + [move_block(UPDATE_PER)] * 4,
        out_shape=[jax.ShapeDtypeStruct(FIELD, F32)]
        + [jax.ShapeDtypeStruct((SHIFT_CAP, HALF * PACK), BF16)] * 4,
        scratch_shapes=[
            pltpu.VMEM((DEV * MSG_OUT, 128), F32),
            pltpu.VMEM((DEV, MSG_OUT, 128), BF16),
            pltpu.SemaphoreType.DMA((PARTS,)),
        ],
        compiler_params=pltpu.CompilerParams(vmem_limit_bytes=60 * 2**20),
        name="update",
    )(scalars, gathered, y_table(), linear, place, stay)


def settle_kernel(scal_ref, base_ref, a0, a1, a2, a3, place_ref, out_ref):
    arrived = jnp.concatenate([a0[...], a1[...], a2[...], a3[...]], axis=0)
    moved = dot(arrived, place_ref[...], ((0,), (0,)))
    keep = scal_ref[2]
    for u, hi in ((u, hi) for u in range(SETTLE_PER) for hi in range(2)):
        for m in range(3):
            for half in range(2):
                start = u * PACK + (hi * 6 + half * 3 + m) * LKX
                out_ref[m, half, hi, u] = (
                    base_ref[m, half, hi, u] + moved[start : start + LKX]
                ) * keep


def settle(scalars, base, arrivals, place):
    return pl.pallas_call(
        settle_kernel,
        grid=(HALF // SETTLE_PER,),
        in_specs=[pl.BlockSpec(memory_space=pltpu.SMEM), field_block(SETTLE_PER)]
        + [move_block(SETTLE_PER)] * 4
        + [pl.BlockSpec((4 * SHIFT_CAP, NY), lambda lo: (0, 0))],
        out_specs=field_block(SETTLE_PER),
        out_shape=jax.ShapeDtypeStruct(FIELD, F32),
        compiler_params=pltpu.CompilerParams(vmem_limit_bytes=16 * 2**20),
        name="settle",
    )(scalars, base, *arrivals, place)


def from_behind(block, axis, distance):
    return lax.ppermute(block, axis, [((i - distance) % COLS, i) for i in range(COLS)])


def local(velocity, register, offsets, remesh_flag, keep_blocks):
    row_index = lax.axis_index("row")
    col_index = lax.axis_index("col")
    moved_by = offsets * remesh_flag
    marked = jnp.stack([moved_by == value for value in OFFSET_VALUES])
    order = jnp.arange(NY, dtype=jnp.int32)
    upto = (order[:, None] <= order[None, :]).astype(BF16)
    ranked = jnp.dot(marked.astype(BF16), upto, preferred_element_type=F32).astype(jnp.int32) - 1
    slots = jnp.arange(SHIFT_CAP, dtype=jnp.int32)
    place = (marked[:, None, :] & (ranked[:, None, :] == slots[None, :, None])).astype(BF16)
    place = place.reshape(4 * SHIFT_CAP, NY)
    stay = (moved_by == 0).astype(F32).reshape(1, NY)
    keep_here = jnp.sum(
        jnp.where(jnp.arange(COLS, dtype=jnp.int32) == col_index, keep_blocks, 0)
    ).astype(F32)
    scalars = jnp.stack(
        [
            (col_index * LKX - NX // 2).astype(F32),
            (row_index * LKZ).astype(F32),
            keep_here,
        ]
    )

    outgoing = y_inverse(velocity)
    table = x_table()
    messages = lax.all_to_all(outgoing, ("row", "col"), split_axis=0, concat_axis=0, tiled=True)
    returning = middle(messages, table)
    gathered = lax.all_to_all(returning, ("row", "col"), split_axis=0, concat_axis=0, tiled=True)
    linear = linear_part(scalars, velocity, register)
    base, *packed = update(scalars, gathered, linear, place, stay)
    arrivals = [
        from_behind(block, "col", value) for block, value in zip(packed, OFFSET_VALUES)
    ]
    sources = [col_index - value for value in OFFSET_VALUES]
    inside = jnp.stack([(source >= 0) & (source < COLS) for source in sources])
    taking = jnp.repeat(inside, SHIFT_CAP)[:, None].astype(BF16) * place
    result = settle(scalars, base, arrivals, taking)
    return result.reshape(velocity.shape)


def solution(mesh):
    placed = (P(None, None, "row", "col", None), P(None, None, "row", "col", None), P(), P(), P())
    return jax.shard_map(
        local,
        mesh=mesh,
        in_specs=placed,
        out_specs=P(None, None, "row", "col", None),
        check_vma=False,
    )
```

time: 177 us -> 157 us (0.89)
  Pallas kernels: 57.2 us -> 42.7 us
  starting transfers between devices: 29.7 us -> 22.1 us
  other arithmetic: 0.84 us -> 2.79 us
    pallas_call x4 -> x5, Pallas kernels: 53.2 us -> 37.4 us  [the longest x1 17.8 us: middle(): pl.pallas_call(middle_kernel, grid=(YPD,), in_specs=[pl.BlockSpec((DEV, M...]
    ppermute x4, starting transfers between devices: 13.2 us -> 5.62 us  [from_behind(): lax.ppermute(block, axis, [((i - distance) % COLS, i) for i in range(COLS)])]
    all_to_all x1, waiting for transfers between devices: 48.4 us -> 42 us  [local(): lax.all_to_all(returning, ('row', 'col'), split_axis=0, concat_axis=0, ti...]
    ppermute x4, waiting for transfers between devices: 6.93 us -> 10.3 us  [from_behind(): lax.ppermute(block, axis, [((i - distance) % COLS, i) for i in range(COLS)])]
  transfers between devices with their start and end apart: 6 -> 6, of which waited for: 4 -> 3; matrix products, arithmetic and copies ran while one was open for 1% -> 2% of each run, Pallas kernels for 2% -> 3%
where the time goes in v2:
time: 157 us; the launch traced here: 155 us
  waiting for transfers between devices  82.6 us (53%)
  Pallas kernels  42.7 us (27%)
  starting transfers between devices  22.1 us (14%)
  local copies, waits for them, and re-layouts  3.73 us (2%)
  other arithmetic  2.79 us (2%)
    all_to_all x1, waiting for transfers between devices, local(): lax.all_to_all(returning, ('row', 'col'), split_axis=0, concat_axis=0, ti...  42 us
    all_to_all x1, waiting for transfers between devices, local(): lax.all_to_all(outgoing, ('row', 'col'), split_axis=0, concat_axis=0, til...  30.3 us
    pallas_call x1, Pallas kernels, middle(): pl.pallas_call(middle_kernel, grid=(YPD,), in_specs=[pl.BlockSpec((DEV, M...  17.8 us
    pallas_call x1, Pallas kernels, update(): pl.pallas_call(update_kernel, grid=(HALF // UPDATE_PER,), in_specs=[pl.Bl...  12 us
    all_to_all x1, starting transfers between devices, local(): lax.all_to_all(outgoing, ('row', 'col'), split_axis=0, concat_axis=0, til...  10.5 us
    ppermute x4, waiting for transfers between devices, from_behind(): lax.ppermute(block, axis, [((i - distance) % COLS, i) for i in range(COLS)])  10.3 us
    all_to_all x1, starting transfers between devices, local(): lax.all_to_all(returning, ('row', 'col'), split_axis=0, concat_axis=0, ti...  6.05 us
    ppermute x4, starting transfers between devices, from_behind(): lax.ppermute(block, axis, [((i - distance) % COLS, i) for i in range(COLS)])  5.62 us
  transfers between devices with their start and end apart: 6, of which 3 were waited for; matrix products, arithmetic and copies ran while one was open for 2% of the time, Pallas kernels for 3%

profile of v2, /device:TPU:8, one launch (start us, length us, event | category | flops | bytes accessed | tf_op | source)
XLA Modules:
  0.0 154.9 jit_solution(4277832886528818186)
XLA Ops:
  0.0 5.3 %y_inverse.1 = bf16[128,72,128]{2,1,0:T(8,128)(2,1)} custom-call(f32[3,2,16,32,256]{4,3,2,1,0:T(8,128)} %v_ref.1, bf16[384,512]{1,0:T(8,128)(2,1)} %constant.55.clone.table_ref), custom_call_target="tpu_custom_call" | custom-call | tf_op jit(solution)/shard_map/y_inverse/pallas_call | solution.py:147
  5.3 10.5 %all-to-all-start = ((bf16[128,72,128]{2,1,0:T(8,128)(2,1)}), bf16[128,72,128]{2,1,0:T(8,128)(2,1)S(1)}, u32[]{:S(2)}, u32[]{:S(2)}) async-start(bf16[128,72,128]{2,1,0:T(8,128)(2,1)} %y_inverse.1), calls=%async_computation | async-start | bytes 4718592 | tf_op jit(solution)/shard_map/all_to_all | solution.py:500
  15.8 0.8 copy-done.5
  16.6 0.7 copy-done.7
  17.3 0.2 x_table.1.x_ref
  17.6 30.3 %all-to-all-done.m_ref = bf16[128,72,128]{2,1,0:T(8,128)(2,1)S(1)} async-done(((bf16[128,72,128]{2,1,0:T(8,128)(2,1)}), bf16[128,72,128]{2,1,0:T(8,128)(2,1)S(1)}, u32[]{:S(2)}, u32[]{:S(2)}) %all-to-all-start) | async-done | bytes 2359328 | tf_op jit(solution)/shard_map/all_to_all | solution.py:500
  47.9 17.8 %middle.1 = bf16[128,120,128]{2,1,0:T(8,128)(2,1)} custom-call(bf16[128,72,128]{2,1,0:T(8,128)(2,1)S(1)} %all-to-all-done.m_ref, bf16[512,768]{1,0:T(8,128)(2,1)S(1)} %x_table.1.x_ref, bf16[384,256]{1,0:T(8,128)(2,1)S(1)} %copy-done.1, bf16[128,208]{1,0:T(8,128)(2,1)S(1)} %copy-done.2, bf16[128,192]{1,0:T(8,128)(2,1)S(1)} %copy-done.3), custom_call_target="tpu_custom_call" | custom-call | tf_op jit(solution)/shard_map/middle/pallas_call | solution.py:277
  65.7 6.1 %all-to-all-start.1 = ((bf16[128,120,128]{2,1,0:T(8,128)(2,1)}), bf16[128,120,128]{2,1,0:T(8,128)(2,1)}, u32[]{:S(2)}, u32[]{:S(2)}) async-start(bf16[128,120,128]{2,1,0:T(8,128)(2,1)} %middle.1), calls=%async_computation.1 | async-start | bytes 7864320 | tf_op jit(solution)/shard_map/all_to_all | solution.py:502
  71.8 0.6 fusion.4
  73.2 0.6 compare_convert_fusion
  73.8 0.2 fusion
  74.0 0.7 fusion.3.place_ref
  74.7 0.6 pad_maximum_fusion.scal_ref
  75.4 4.6 %linear.1.lin_ref = f32[3,2,2,8,32,256]{5,4,3,2,1,0:T(8,128)} custom-call(f32[3]{0:T(128)} %pad_maximum_fusion.scal_ref, f32[3,2,2,8,32,256]{5,4,3,2,1,0:T(8,128)} %bitcast.26, f32[3,2,2,8,32,256]{5,4,3,2,1,0:T(8,128)} %bitcast.27), custom_call_target="tpu_custom_call" | custom-call | tf_op jit(solution)/shard_map/linear/pallas_call | solution.py:343
  79.9 42.0 %all-to-all-done.1.g_hbm = bf16[128,120,128]{2,1,0:T(8,128)(2,1)} async-done(((bf16[128,120,128]{2,1,0:T(8,128)(2,1)}), bf16[128,120,128]{2,1,0:T(8,128)(2,1)}, u32[]{:S(2)}, u32[]{:S(2)}) %all-to-all-start.1) | async-done | bytes 3932192 | tf_op jit(solution)/shard_map/all_to_all | solution.py:502
  122.0 12.0 %update.1 = (f32[3,2,2,8,32,256]{5,4,3,2,1,0:T(8,128)}, bf16[32,3072]{1,0:T(8,128)(2,1)}, bf16[32,3072]{1,0:T(8,128)(2,1)}, bf16[32,3072]{1,0:T(8,128)(2,1)}, bf16[32,3072]{1,0:T(8,128)(2,1)}) custom-call(f32[3]{0:T(128)} %pad_maximum_fusion.scal_ref, bf16[128,120,128]{2,1,0:T(8,128)(2,1)} %all-to-all-done.1.g_hbm, ...), custom_call_target="tpu_custom_call" | custom-call | tf_op jit(solution)/shard_map/update/pallas_call | solution.py:420
  134.1 2.4 %collective-permute-start.1 = (bf16[32,3072]{1,0:T(8,128)(2,1)}, bf16[32,3072]{1,0:T(8,128)(2,1)S(1)}, u32[]{:S(2)}, u32[]{:S(2)}) collective-permute-start(bf16[32,3072]{1,0:T(8,128)(2,1)} %get-tuple-element.12), channel_id=1, source_target_pairs={{1,0},{2,1},{3,2},{4,3},{5,4},{6,5},{7,6},{8,7},{9,8},{10,9},{11,1... | collective-permute-start | bytes 589832 | tf_op jit(solution)/shard_map/ppermute | solution.py:472
  136.5 0.8 collective-permute-start.2
  137.2 2.4 %collective-permute-start.3 = (bf16[32,3072]{1,0:T(8,128)(2,1)}, bf16[32,3072]{1,0:T(8,128)(2,1)S(1)}, u32[]{:S(2)}, u32[]{:S(2)}) collective-permute-start(bf16[32,3072]{1,0:T(8,128)(2,1)} %get-tuple-element.14), channel_id=1, source_target_pairs={{14,0},{15,1},{0,2},{1,3},{2,4},{3,5},{4,6},{5,7},{6,8},{7,9},{8,1... | collective-permute-start | bytes 589832 | tf_op jit(solution)/shard_map/ppermute | solution.py:472
  139.8 0.1 convert_element_type.37
  139.9 0.1 fusion.2.place_ref
  140.0 10.3 %collective-permute-done.a0 = bf16[32,3072]{1,0:T(8,128)(2,1)S(1)} collective-permute-done((bf16[32,3072]{1,0:T(8,128)(2,1)}, bf16[32,3072]{1,0:T(8,128)(2,1)S(1)}, u32[]{:S(2)}, u32[]{:S(2)}) %collective-permute-start) | collective-permute-done | bytes 196640 | tf_op jit(solution)/shard_map/ppermute | solution.py:472
  150.3 1.9 %copy-done = f32[3,2,2,8,32,256]{5,4,3,2,1,0:T(8,128)S(1)} copy-done((f32[3,2,2,8,32,256]{5,4,3,2,1,0:T(8,128)S(1)}, f32[3,2,2,8,32,256]{5,4,3,2,1,0:T(8,128)}, u32[]{:S(2)}) %copy-start) | copy-done | bytes 3145752
  152.2 2.7 %settle.1 = f32[3,2,2,8,32,256]{5,4,3,2,1,0:T(8,128)} custom-call(f32[3]{0:T(128)S(1)} %copy-done.8, f32[3,2,2,8,32,256]{5,4,3,2,1,0:T(8,128)S(1)} %copy-done, bf16[32,3072]{1,0:T(8,128)(2,1)S(1)} %collective-permute-done.a0, bf16[32,3072]{1,0:T(8,128)(2,1)S(1)} %collective-permute-done.1.a1, bf16[32,3072]{1,0:T(8,128)(2,1)S(1)} %collective-permute-done.2.a2, ...), custom_call_target="tpu_custom_call" | custom-call | tf_op jit(solution)/shard_map/settle/pallas_call | solution.py:458
  (35 shorter events, 0.4 us)
Async XLA Ops:
  5.3 10.5 %copy-start.4 = (f32[32,384]{1,0:T(8,128)S(1)}, f32[32,384]{1,0:T(8,128)}, u32[]{:S(2)}) copy-start(f32[32,384]{1,0:T(8,128)} %constant.58.clone.fine_cos) | copy-start | bytes 147460
  5.3 10.5 %copy-start.6 = (f32[16,384]{1,0:T(8,128)S(1)}, f32[16,384]{1,0:T(8,128)}, u32[]{:S(2)}) copy-start(f32[16,384]{1,0:T(8,128)} %constant.56.clone.coarse_cos) | copy-start | bytes 73732
  5.3 42.6 %copy-start.1 = (bf16[384,256]{1,0:T(8,128)(2,1)S(1)}, bf16[384,256]{1,0:T(8,128)(2,1)}, u32[]{:S(2)}) copy-start(bf16[384,256]{1,0:T(8,128)(2,1)} %constant.60.clone.zi_ref) | copy-start | bytes 589828
  5.3 42.6 %copy-start.2 = (bf16[128,208]{1,0:T(8,128)(2,1)S(1)}, bf16[128,208]{1,0:T(8,128)(2,1)}, u32[]{:S(2)}) copy-start(bf16[128,208]{1,0:T(8,128)(2,1)} %constant.61.clone.zr_ref) | copy-start | bytes 159748
  5.3 42.6 %copy-start.3 = (bf16[128,192]{1,0:T(8,128)(2,1)S(1)}, bf16[128,192]{1,0:T(8,128)(2,1)}, u32[]{:S(2)}) copy-start(bf16[128,192]{1,0:T(8,128)(2,1)} %constant.62.clone.zm_ref) | copy-start | bytes 147460
  5.3 42.6 %all-to-all-start = ((bf16[128,72,128]{2,1,0:T(8,128)(2,1)}), bf16[128,72,128]{2,1,0:T(8,128)(2,1)S(1)}, u32[]{:S(2)}, u32[]{:S(2)}) async-start(bf16[128,72,128]{2,1,0:T(8,128)(2,1)} %y_inverse.1), calls=%async_computation | async-start | bytes 4718592 | tf_op jit(solution)/shard_map/all_to_all | solution.py:500
  15.8 0.8 copy-start.5
  16.6 0.7 copy-start.7
  65.7 6.1 %copy-start.11 = (s32[16]{0:T(128)S(1)}, s32[16]{0:T(128)}, u32[]{:S(2)}) copy-start(s32[16]{0:T(128)} %param.18) | copy-start | bytes 196
  65.7 7.5 %copy-start.9 = (s32[256]{0:T(256)S(1)}, s32[256]{0:T(256)}, u32[]{:S(2)}) copy-start(s32[256]{0:T(256)} %param.16) | copy-start | bytes 3076
  65.7 7.5 %copy-start.10 = (s32[256]{0:T(256)S(1)}, s32[256]{0:T(256)}, u32[]{:S(2)}) copy-start(s32[256]{0:T(256)} %param.17) | copy-start | bytes 3076
  65.7 56.3 %all-to-all-start.1 = ((bf16[128,120,128]{2,1,0:T(8,128)(2,1)}), bf16[128,120,128]{2,1,0:T(8,128)(2,1)}, u32[]{:S(2)}, u32[]{:S(2)}) async-start(bf16[128,120,128]{2,1,0:T(8,128)(2,1)} %middle.1), calls=%async_computation.1 | async-start | bytes 7864320 | tf_op jit(solution)/shard_map/all_to_all | solution.py:502
  122.0 28.3 %copy-start.8 = (f32[3]{0:T(128)S(1)}, f32[3]{0:T(128)}, u32[]{:S(2)}) copy-start(f32[3]{0:T(128)} %pad_maximum_fusion.scal_ref) | copy-start | bytes 40
  134.0 16.3 %collective-permute-start = (bf16[32,3072]{1,0:T(8,128)(2,1)}, bf16[32,3072]{1,0:T(8,128)(2,1)S(1)}, u32[]{:S(2)}, u32[]{:S(2)}) collective-permute-start(bf16[32,3072]{1,0:T(8,128)(2,1)} %get-tuple-element.11), channel_id=1, source_target_pairs={{2,0},{3,1},{4,2},{5,3},{6,4},{7,5},{8,6},{9,7},{10,8},{11,9},{12,... | collective-permute-start | bytes 589832 | tf_op jit(solution)/shard_map/ppermute | solution.py:472
  134.1 16.2 %collective-permute-start.1 = (bf16[32,3072]{1,0:T(8,128)(2,1)}, bf16[32,3072]{1,0:T(8,128)(2,1)S(1)}, u32[]{:S(2)}, u32[]{:S(2)}) collective-permute-start(bf16[32,3072]{1,0:T(8,128)(2,1)} %get-tuple-element.12), channel_id=1, source_target_pairs={{1,0},{2,1},{3,2},{4,3},{5,4},{6,5},{7,6},{8,7},{9,8},{10,9},{11,1... | collective-permute-start | bytes 589832 | tf_op jit(solution)/shard_map/ppermute | solution.py:472
  136.5 13.8 %collective-permute-start.2 = (bf16[32,3072]{1,0:T(8,128)(2,1)}, bf16[32,3072]{1,0:T(8,128)(2,1)S(1)}, u32[]{:S(2)}, u32[]{:S(2)}) collective-permute-start(bf16[32,3072]{1,0:T(8,128)(2,1)} %get-tuple-element.13), channel_id=1, source_target_pairs={{15,0},{0,1},{1,2},{2,3},{3,4},{4,5},{5,6},{6,7},{7,8},{8,9},{9,10... | collective-permute-start | bytes 589832 | tf_op jit(solution)/shard_map/ppermute | solution.py:472
  137.2 13.0 %collective-permute-start.3 = (bf16[32,3072]{1,0:T(8,128)(2,1)}, bf16[32,3072]{1,0:T(8,128)(2,1)S(1)}, u32[]{:S(2)}, u32[]{:S(2)}) collective-permute-start(bf16[32,3072]{1,0:T(8,128)(2,1)} %get-tuple-element.14), channel_id=1, source_target_pairs={{14,0},{15,1},{0,2},{1,3},{2,4},{3,5},{4,6},{5,7},{6,8},{7,9},{8,1... | collective-permute-start | bytes 589832 | tf_op jit(solution)/shard_map/ppermute | solution.py:472
  150.3 1.9 %copy-start = (f32[3,2,2,8,32,256]{5,4,3,2,1,0:T(8,128)S(1)}, f32[3,2,2,8,32,256]{5,4,3,2,1,0:T(8,128)}, u32[]{:S(2)}) copy-start(f32[3,2,2,8,32,256]{5,4,3,2,1,0:T(8,128)} %get-tuple-element.10.base_ref) | copy-start | bytes 9437188

commit v3 on v2

--- a/solution.py
+++ b/solution.py
@@ -183,7 +183,9 @@
     return lanes < 64, lax.rem(lanes, 64) < 32
 
 
-def middle_kernel(m_ref, x_ref, zi_ref, zr_ref, zm_ref, o_ref, u_ref, f_ref):
+def middle_kernel(
+    m_ref, x_ref, zi_ref, zr_ref, zm_ref, o_ref, u_ref, f_ref, w_ref, d_ref, t_ref
+):
     y = pl.program_id(0)
     rows_of_y = [
         pl.ds(pl.multiple_of(c * GROUPS + y * HALF, HALF), HALF) for c in range(3)
@@ -205,53 +207,64 @@
                 for c in range(3):
                     rows = slice(c * HALF, (c + 1) * HALF)
                     both = jnp.concatenate([parts[s][rows], parts[2 + s][rows]], axis=0)
-                    start = (s * 3 + c) * NZH + r * LKZ
+                    start = (c * 2 + s) * NZH + r * LKZ
                     u_ref[start : start + LKZ, cg * 128 : (cg + 1) * 128] = both.astype(BF16)
 
     zi = zi_ref[...]
     zr = zr_ref[...]
     zm = zm_ref[...]
-    first = lax.broadcasted_iota(jnp.int32, (NZH, 128), 1) == 0
+    first = lax.broadcasted_iota(jnp.int32, (LKZ, 128), 1) == 0
     half = MZ // 2
+    for c in range(3):
+        res = dot(u_ref[c * 2 * NZH : (c + 1) * 2 * NZH], x_ref[...], ((1,), (0,)))
+        for n in range(XN):
+            cos_at = slice(n * 256, n * 256 + 128)
+            sin_at = slice(n * 256 + 128, (n + 1) * 256)
+            for k in range(0, NZH, LKZ):
+                top = slice(k, k + LKZ)
+                bottom = slice(NZH + k, NZH + k + LKZ)
+                cr, sr = res[top, cos_at], res[top, sin_at]
+                ci, si = res[bottom, cos_at], res[bottom, sin_at]
+                x1, x2 = si, sr
+                if n == 0:
+                    x1 = jnp.where(first, -sr, si)
+                    x2 = jnp.where(first, si, sr)
+                w_ref[c, top, cos_at] = (cr - x1).astype(BF16)
+                w_ref[c, top, sin_at] = (cr + x1).astype(BF16)
+                w_ref[c, bottom, cos_at] = (ci + x2).astype(BF16)
+                w_ref[c, bottom, sin_at] = (ci - x2).astype(BF16)
+        d_ref[c] = dot(zi, w_ref[c], ((1,), (0,)))
     for n in range(XN):
         here = slice(n * 256, (n + 1) * 256)
-        res = dot(u_ref[...], x_ref[:, here], ((1,), (0,)))
-        fields = []
-        for c in range(3):
-            top = slice(c * NZH, (c + 1) * NZH)
-            bottom = slice((3 + c) * NZH, (4 + c) * NZH)
-            cr, sr = res[top, :128], res[top, 128:]
-            ci, si = res[bottom, :128], res[bottom, 128:]
-            x1, x2 = si, sr
-            if n == 0:
-                x1 = jnp.where(first, -sr, si)
-                x2 = jnp.where(first, si, sr)
-            modes = jnp.concatenate(
-                [
-                    jnp.concatenate([cr - x1, cr + x1], axis=1),
-                    jnp.concatenate([ci + x2, ci - x2], axis=1),
-                ],
-                axis=0,
-            ).astype(BF16)
-            fields.append(dot(zi, modes, ((1,), (0,))))
-        f0, f1, f2 = fields
-        last = f2 * f2
-        products = (f0 * f0 - last, f0 * f1, f0 * f2, f1 * f1 - last, f1 * f2)
-        for e, product in enumerate(products):
-            even = (product[:half] + product[half:]).astype(BF16)
-            odd = (product[:half] - product[half:]).astype(BF16)
-            mr = dot(zr, jnp.concatenate([even, odd[:16]], axis=0), ((1,), (0,)))
-            mi = dot(zm, odd, ((1,), (0,)))
-            er, orr = mr[:, :128] + mr[:, 128:], mr[:, :128] - mr[:, 128:]
-            ei, oi = mi[:, :128] + mi[:, 128:], mi[:, :128] - mi[:, 128:]
-            x1, x2 = oi, -orr
-            if n == 0:
-                x1 = jnp.where(first, orr, oi)
-                x2 = jnp.where(first, oi, -orr)
-            top = slice(e * NZH, (e + 1) * NZH)
-            bottom = slice((PRODUCTS + e) * NZH, (PRODUCTS + e + 1) * NZH)
-            f_ref[top, here] = jnp.concatenate([er, x1], axis=1).astype(BF16)
-            f_ref[bottom, here] = jnp.concatenate([ei, x2], axis=1).astype(BF16)
+        for k in range(0, half, LKZ):
+            pair = []
+            for start in (k, half + k):
+                f0, f1, f2 = [d_ref[c, start : start + LKZ, here] for c in range(3)]
+                last = f2 * f2
+                pair.append((f0 * f0 - last, f0 * f1, f0 * f2, f1 * f1 - last, f1 * f2))
+            for e in range(PRODUCTS):
+                t_ref[e, k : k + LKZ, here] = (pair[0][e] + pair[1][e]).astype(BF16)
+                t_ref[e, half + k : half + k + LKZ, here] = (pair[0][e] - pair[1][e]).astype(BF16)
+    for e in range(PRODUCTS):
+        mr = dot(zr, t_ref[e, : half + LKZ], ((1,), (0,)))
+        mi = dot(zm, t_ref[e, half:], ((1,), (0,)))
+        for n in range(XN):
+            cos_at = slice(n * 256, n * 256 + 128)
+            sin_at = slice(n * 256 + 128, (n + 1) * 256)
+            for k in range(0, NZH, LKZ):
+                rows = slice(k, k + LKZ)
+                er, orr = mr[rows, cos_at] + mr[rows, sin_at], mr[rows, cos_at] - mr[rows, sin_at]
+                ei, oi = mi[rows, cos_at] + mi[rows, sin_at], mi[rows, cos_at] - mi[rows, sin_at]
+                x1, x2 = oi, -orr
+                if n == 0:
+                    x1 = jnp.where(first, orr, oi)
+                    x2 = jnp.where(first, oi, -orr)
+                top = slice(e * NZH + k, e * NZH + k + LKZ)
+                bottom = slice((PRODUCTS + e) * NZH + k, (PRODUCTS + e) * NZH + k + LKZ)
+                f_ref[top, cos_at] = er.astype(BF16)
+                f_ref[top, sin_at] = x1.astype(BF16)
+                f_ref[bottom, cos_at] = ei.astype(BF16)
+                f_ref[bottom, sin_at] = x2.astype(BF16)
 
     masks = lane_masks(PRODUCTS * HALF)
     for m in range(NX // 256):
@@ -289,6 +302,9 @@
         scratch_shapes=[
             pltpu.VMEM((6 * NZH, NX), BF16),
             pltpu.VMEM((2 * PRODUCTS * NZH, MX), BF16),
+            pltpu.VMEM((3, 2 * NZH, MX), BF16),
+            pltpu.VMEM((3, MZ, MX), F32),
+            pltpu.VMEM((PRODUCTS, MZ, MX), BF16),
         ],
         compiler_params=pltpu.CompilerParams(vmem_limit_bytes=26 * 2**20),
         name="middle",
@@ -304,10 +320,15 @@
     return pl.BlockSpec((3, 2, 2, per, LKX, NY), lambda k: (0, 0, 0, k, 0, 0))
 
 
+def slab_block(per):
+    return pl.BlockSpec((1, 3, 2, 2, per, LKX, NY), lambda k: (0, 0, 0, 0, k, 0, 0))
+
+
 def move_block(per):
     return pl.BlockSpec((SHIFT_CAP, per * PACK), lambda k: (0, k))
 
 
+SLABS = 8
 LINEAR_PER = 4
 UPDATE_PER = 2
 SETTLE_PER = 4
@@ -336,7 +357,7 @@
                 if m == 1:
                     rate = rate - SHEAR_RATE * first
                 increment = REGISTER_WEIGHT * reg_ref[m, half, hi, u] + TIME_STEP * rate
-                out_ref[m, half, hi, u] = velocity + UPDATE_WEIGHT * increment
+                out_ref[0, m, half, hi, u] = velocity + UPDATE_WEIGHT * increment
 
 
 def linear_part(scalars, velocity, register):
@@ -344,8 +365,8 @@
         linear_kernel,
         grid=(HALF // LINEAR_PER,),
         in_specs=[pl.BlockSpec(memory_space=pltpu.SMEM), field_block(LINEAR_PER), field_block(LINEAR_PER)],
-        out_specs=field_block(LINEAR_PER),
-        out_shape=pltpu.HBM(FIELD, F32),
+        out_specs=slab_block(LINEAR_PER),
+        out_shape=pltpu.HBM((SLABS,) + FIELD, F32),
         compiler_params=pltpu.CompilerParams(vmem_limit_bytes=60 * 2**20),
         name="linear",
     )(scalars, velocity.reshape(FIELD), register.reshape(FIELD))
@@ -408,7 +429,7 @@
                 )
                 pressure = (k1 * stress[0] + k2 * stress[1] + k3 * stress[2]) * inverse
                 for m, wave in enumerate((k1, k2, k3)):
-                    updated = lin_ref[m, half, hi, u] + sign * (stress[m] - wave * pressure)
+                    updated = lin_ref[0, m, half, hi, u] + sign * (stress[m] - wave * pressure)
                     base_ref[m, half, hi, u] = updated * stay
                     moving.append(updated.astype(BF16))
         packed = dot(place_ref[...], jnp.concatenate(moving, axis=0), ((1,), (1,))).astype(BF16)
@@ -424,7 +445,7 @@
             pl.BlockSpec(memory_space=pltpu.SMEM),
             pl.BlockSpec(memory_space=pl.ANY),
             pl.BlockSpec((MY, 2 * NY), lambda lo: (0, 0)),
-            field_block(UPDATE_PER),
+            slab_block(UPDATE_PER),
             pl.BlockSpec((4 * SHIFT_CAP, NY), lambda lo: (0, 0)),
             pl.BlockSpec((1, NY), lambda lo: (0, 0)),
         ],
@@ -436,7 +457,7 @@
             pltpu.VMEM((DEV, MSG_OUT, 128), BF16),
             pltpu.SemaphoreType.DMA((PARTS,)),
         ],
-        compiler_params=pltpu.CompilerParams(vmem_limit_bytes=60 * 2**20),
+        compiler_params=pltpu.CompilerParams(vmem_limit_bytes=44 * 2**20),
         name="update",
     )(scalars, gathered, y_table(), linear, place, stay)
 

time: 157 us -> 153 us (0.975)
  Pallas kernels: 42.7 us -> 40 us
    pallas_call x1, Pallas kernels: 17.8 us -> 15.1 us  [middle(): pl.pallas_call(middle_kernel, grid=(YPD,), in_specs=[pl.BlockSpec((DEV, M...]
    ppermute x4, waiting for transfers between devices: 10.3 us -> 8.39 us  [from_behind(): lax.ppermute(block, axis, [((i - distance) % COLS, i) for i in range(COLS)])]
    unnamed x24 -> x28, local copies, waits for them, and re-layouts: 3.45 us -> 2.42 us
  transfers between devices with their start and end apart: 6 -> 6, of which waited for: 3 -> 3; matrix products, arithmetic and copies ran while one was open for 2% -> 3% of each run, Pallas kernels for 3% -> 3%
where the time goes in v3:
time: 153 us; the launch traced here: 151 us
  waiting for transfers between devices  81.2 us (53%)
  Pallas kernels  40 us (26%)
  starting transfers between devices  22.1 us (14%)
  local copies, waits for them, and re-layouts  3.95 us (3%)
  other arithmetic  2.87 us (2%)
    all_to_all x1, waiting for transfers between devices, local(): lax.all_to_all(returning, ('row', 'col'), split_axis=0, concat_axis=0, ti...  42.5 us
    all_to_all x1, waiting for transfers between devices, local(): lax.all_to_all(outgoing, ('row', 'col'), split_axis=0, concat_axis=0, til...  30.3 us
    pallas_call x1, Pallas kernels, middle(): pl.pallas_call(middle_kernel, grid=(YPD,), in_specs=[pl.BlockSpec((DEV, M...  15.1 us
    pallas_call x1, Pallas kernels, update(): pl.pallas_call(update_kernel, grid=(HALF // UPDATE_PER,), in_specs=[pl.Bl...  11.6 us
    all_to_all x1, starting transfers between devices, local(): lax.all_to_all(outgoing, ('row', 'col'), split_axis=0, concat_axis=0, til...  10.5 us
    ppermute x4, waiting for transfers between devices, from_behind(): lax.ppermute(block, axis, [((i - distance) % COLS, i) for i in range(COLS)])  8.39 us
    all_to_all x1, starting transfers between devices, local(): lax.all_to_all(returning, ('row', 'col'), split_axis=0, concat_axis=0, ti...  6.04 us
    ppermute x4, starting transfers between devices, from_behind(): lax.ppermute(block, axis, [((i - distance) % COLS, i) for i in range(COLS)])  5.62 us
  transfers between devices with their start and end apart: 6, of which 3 were waited for; matrix products, arithmetic and copies ran while one was open for 3% of the time, Pallas kernels for 3%

profile of v3, /device:TPU:8, one launch (start us, length us, event | category | flops | bytes accessed | tf_op | source)
XLA Modules:
  0.0 151.1 jit_solution(11536244905973882924)
XLA Ops:
  0.0 5.3 %y_inverse.1 = bf16[128,72,128]{2,1,0:T(8,128)(2,1)} custom-call(f32[3,2,16,32,256]{4,3,2,1,0:T(8,128)} %v_ref.1, bf16[384,512]{1,0:T(8,128)(2,1)} %constant.55.clone.table_ref), custom_call_target="tpu_custom_call" | custom-call | tf_op jit(solution)/shard_map/y_inverse/pallas_call | solution.py:147
  5.3 10.5 %all-to-all-start = ((bf16[128,72,128]{2,1,0:T(8,128)(2,1)}), bf16[128,72,128]{2,1,0:T(8,128)(2,1)S(1)}, u32[]{:S(2)}, u32[]{:S(2)}) async-start(bf16[128,72,128]{2,1,0:T(8,128)(2,1)} %y_inverse.1), calls=%async_computation | async-start | bytes 4718592 | tf_op jit(solution)/shard_map/all_to_all | solution.py:521
  15.8 0.8 copy-done.6
  16.6 0.7 copy-done.8
  17.3 0.2 x_table.1.x_ref
  17.6 30.3 %all-to-all-done.m_ref = bf16[128,72,128]{2,1,0:T(8,128)(2,1)S(1)} async-done(((bf16[128,72,128]{2,1,0:T(8,128)(2,1)}), bf16[128,72,128]{2,1,0:T(8,128)(2,1)S(1)}, u32[]{:S(2)}, u32[]{:S(2)}) %all-to-all-start) | async-done | bytes 2359328 | tf_op jit(solution)/shard_map/all_to_all | solution.py:521
  47.9 15.1 %middle.1 = bf16[128,120,128]{2,1,0:T(8,128)(2,1)} custom-call(bf16[128,72,128]{2,1,0:T(8,128)(2,1)S(1)} %all-to-all-done.m_ref, bf16[512,768]{1,0:T(8,128)(2,1)S(1)} %x_table.1.x_ref, bf16[384,256]{1,0:T(8,128)(2,1)S(1)} %copy-done.2, bf16[128,208]{1,0:T(8,128)(2,1)S(1)} %copy-done.3, bf16[128,192]{1,0:T(8,128)(2,1)S(1)} %copy-done.4), custom_call_target="tpu_custom_call" | custom-call | tf_op jit(solution)/shard_map/middle/pallas_call | solution.py:290
  63.0 6.0 %all-to-all-start.1 = ((bf16[128,120,128]{2,1,0:T(8,128)(2,1)}), bf16[128,120,128]{2,1,0:T(8,128)(2,1)}, u32[]{:S(2)}, u32[]{:S(2)}) async-start(bf16[128,120,128]{2,1,0:T(8,128)(2,1)} %middle.1), calls=%async_computation.1 | async-start | bytes 7864320 | tf_op jit(solution)/shard_map/all_to_all | solution.py:523
  69.1 0.6 fusion.4
  70.6 0.2 fusion
  70.7 0.7 fusion.3.place_ref
  71.4 0.6 pad_maximum_fusion.scal_ref
  72.1 4.7 %linear.1.lin_ref = f32[8,3,2,2,8,32,256]{6,5,4,3,2,1,0:T(8,128)} custom-call(f32[3]{0:T(128)} %pad_maximum_fusion.scal_ref, f32[3,2,2,8,32,256]{5,4,3,2,1,0:T(8,128)} %bitcast.27, f32[3,2,2,8,32,256]{5,4,3,2,1,0:T(8,128)} %bitcast.28), custom_call_target="tpu_custom_call" | custom-call | tf_op jit(solution)/shard_map/linear/pallas_call | solution.py:364
  76.8 42.5 %all-to-all-done.1.g_hbm = bf16[128,120,128]{2,1,0:T(8,128)(2,1)} async-done(((bf16[128,120,128]{2,1,0:T(8,128)(2,1)}), bf16[128,120,128]{2,1,0:T(8,128)(2,1)}, u32[]{:S(2)}, u32[]{:S(2)}) %all-to-all-start.1) | async-done | bytes 3932192 | tf_op jit(solution)/shard_map/all_to_all | solution.py:523
  119.3 0.8 copy-done.1
  120.1 11.6 %update.1 = (f32[3,2,2,8,32,256]{5,4,3,2,1,0:T(8,128)S(1)}, bf16[32,3072]{1,0:T(8,128)(2,1)}, bf16[32,3072]{1,0:T(8,128)(2,1)}, bf16[32,3072]{1,0:T(8,128)(2,1)}, bf16[32,3072]{1,0:T(8,128)(2,1)}) custom-call(f32[3]{0:T(128)S(1)} %copy-done.9, bf16[128,120,128]{2,1,0:T(8,128)(2,1)} %all-to-all-done.1.g_hbm, bf16[384,512]{1,0:T(8,128)(2,1)S(1)} %copy-done, ...), custom_call_target="tpu_custom_call" | custom-call | tf_op jit(solution)/shard_map/update/pallas_call | solution.py:441
  131.8 2.4 %collective-permute-start.1 = (bf16[32,3072]{1,0:T(8,128)(2,1)}, bf16[32,3072]{1,0:T(8,128)(2,1)S(1)}, u32[]{:S(2)}, u32[]{:S(2)}) collective-permute-start(bf16[32,3072]{1,0:T(8,128)(2,1)} %get-tuple-element.12), channel_id=1, source_target_pairs={{1,0},{2,1},{3,2},{4,3},{5,4},{6,5},{7,6},{8,7},{9,8},{10,9},{11,1... | collective-permute-start | bytes 589832 | tf_op jit(solution)/shard_map/ppermute | solution.py:493
  134.2 0.8 collective-permute-start.2
  134.9 2.4 %collective-permute-start.3 = (bf16[32,3072]{1,0:T(8,128)(2,1)}, bf16[32,3072]{1,0:T(8,128)(2,1)}, u32[]{:S(2)}, u32[]{:S(2)}) collective-permute-start(bf16[32,3072]{1,0:T(8,128)(2,1)} %get-tuple-element.14), channel_id=1, source_target_pairs={{14,0},{15,1},{0,2},{1,3},{2,4},{3,5},{4,6},{5,7},{6,8},{7,9},{8,1... | collective-permute-start | bytes 589832 | tf_op jit(solution)/shard_map/ppermute | solution.py:493
  137.4 0.7 broadcast_in_dim.7
  138.1 0.8 convert_element_type.37
  138.8 0.8 fusion.2.place_ref
  139.6 8.4 %collective-permute-done.a0 = bf16[32,3072]{1,0:T(8,128)(2,1)S(1)} collective-permute-done((bf16[32,3072]{1,0:T(8,128)(2,1)}, bf16[32,3072]{1,0:T(8,128)(2,1)S(1)}, u32[]{:S(2)}, u32[]{:S(2)}) %collective-permute-start) | collective-permute-done | bytes 196640 | tf_op jit(solution)/shard_map/ppermute | solution.py:493
  148.0 3.2 %settle.1 = f32[3,2,2,8,32,256]{5,4,3,2,1,0:T(8,128)} custom-call(f32[3]{0:T(128)S(1)} %copy-done.9, f32[3,2,2,8,32,256]{5,4,3,2,1,0:T(8,128)S(1)} %get-tuple-element.10.base_ref, bf16[32,3072]{1,0:T(8,128)(2,1)S(1)} %collective-permute-done.a0, bf16[32,3072]{1,0:T(8,128)(2,1)S(1)} %collective-permute-done.1.a1, bf16[32,3072]{1,0:T(8,128)(2,1)} %collective-permute-done.2.a2, ...), custom_call_target="tpu_custom_call" | custom-call | tf_op jit(solution)/shard_map/settle/pallas_call | solution.py:479
  (39 shorter events, 0.4 us)
Async XLA Ops:
  5.3 10.5 %copy-start.5 = (f32[32,384]{1,0:T(8,128)S(1)}, f32[32,384]{1,0:T(8,128)}, u32[]{:S(2)}) copy-start(f32[32,384]{1,0:T(8,128)} %constant.58.clone.fine_cos) | copy-start | bytes 147460
  5.3 10.5 %copy-start.7 = (f32[16,384]{1,0:T(8,128)S(1)}, f32[16,384]{1,0:T(8,128)}, u32[]{:S(2)}) copy-start(f32[16,384]{1,0:T(8,128)} %constant.56.clone.coarse_cos) | copy-start | bytes 73732
  5.3 42.6 %copy-start.2 = (bf16[384,256]{1,0:T(8,128)(2,1)S(1)}, bf16[384,256]{1,0:T(8,128)(2,1)}, u32[]{:S(2)}) copy-start(bf16[384,256]{1,0:T(8,128)(2,1)} %constant.60.clone.zi_ref) | copy-start | bytes 589828
  5.3 42.6 %copy-start.3 = (bf16[128,208]{1,0:T(8,128)(2,1)S(1)}, bf16[128,208]{1,0:T(8,128)(2,1)}, u32[]{:S(2)}) copy-start(bf16[128,208]{1,0:T(8,128)(2,1)} %constant.61.clone.zr_ref) | copy-start | bytes 159748
  5.3 42.6 %copy-start.4 = (bf16[128,192]{1,0:T(8,128)(2,1)S(1)}, bf16[128,192]{1,0:T(8,128)(2,1)}, u32[]{:S(2)}) copy-start(bf16[128,192]{1,0:T(8,128)(2,1)} %constant.62.clone.zm_ref) | copy-start | bytes 147460
  5.3 42.6 %all-to-all-start = ((bf16[128,72,128]{2,1,0:T(8,128)(2,1)}), bf16[128,72,128]{2,1,0:T(8,128)(2,1)S(1)}, u32[]{:S(2)}, u32[]{:S(2)}) async-start(bf16[128,72,128]{2,1,0:T(8,128)(2,1)} %y_inverse.1), calls=%async_computation | async-start | bytes 4718592 | tf_op jit(solution)/shard_map/all_to_all | solution.py:521
  15.8 0.8 copy-start.6
  16.6 0.7 copy-start.8
  63.0 6.1 %copy-start.13 = (s32[16]{0:T(128)S(1)}, s32[16]{0:T(128)}, u32[]{:S(2)}) copy-start(s32[16]{0:T(128)} %param.18) | copy-start | bytes 196
  63.0 7.5 %copy-start.11 = (s32[256]{0:T(256)S(1)}, s32[256]{0:T(256)}, u32[]{:S(2)}) copy-start(s32[256]{0:T(256)} %param.16) | copy-start | bytes 3076
  63.0 7.5 %copy-start.12 = (s32[256]{0:T(256)S(1)}, s32[256]{0:T(256)}, u32[]{:S(2)}) copy-start(s32[256]{0:T(256)} %param.17) | copy-start | bytes 3076
  63.0 56.3 %all-to-all-start.1 = ((bf16[128,120,128]{2,1,0:T(8,128)(2,1)}), bf16[128,120,128]{2,1,0:T(8,128)(2,1)}, u32[]{:S(2)}, u32[]{:S(2)}) async-start(bf16[128,120,128]{2,1,0:T(8,128)(2,1)} %middle.1), calls=%async_computation.1 | async-start | bytes 7864320 | tf_op jit(solution)/shard_map/all_to_all | solution.py:523
  70.5 1.6 %copy-start.10 = (s32[128]{0:T(128)}, s32[128]{0:T(128)S(1)}, u32[]{:S(2)}) copy-start(s32[128]{0:T(128)S(1)} %eq.69) | copy-start | bytes 1540
  72.1 47.2 %copy-start = (bf16[384,512]{1,0:T(8,128)(2,1)S(1)}, bf16[384,512]{1,0:T(8,128)(2,1)}, u32[]{:S(2)}) copy-start(bf16[384,512]{1,0:T(8,128)(2,1)} %constant.55.clone.table_ref) | copy-start | bytes 1179652
  72.1 47.2 %copy-start.9 = (f32[3]{0:T(128)S(1)}, f32[3]{0:T(128)}, u32[]{:S(2)}) copy-start(f32[3]{0:T(128)} %pad_maximum_fusion.scal_ref) | copy-start | bytes 40
  119.3 0.8 copy-start.1
  131.7 16.3 %collective-permute-start = (bf16[32,3072]{1,0:T(8,128)(2,1)}, bf16[32,3072]{1,0:T(8,128)(2,1)S(1)}, u32[]{:S(2)}, u32[]{:S(2)}) collective-permute-start(bf16[32,3072]{1,0:T(8,128)(2,1)} %get-tuple-element.11), channel_id=1, source_target_pairs={{2,0},{3,1},{4,2},{5,3},{6,4},{7,5},{8,6},{9,7},{10,8},{11,9},{12,... | collective-permute-start | bytes 589832 | tf_op jit(solution)/shard_map/ppermute | solution.py:493
  131.8 16.2 %collective-permute-start.1 = (bf16[32,3072]{1,0:T(8,128)(2,1)}, bf16[32,3072]{1,0:T(8,128)(2,1)S(1)}, u32[]{:S(2)}, u32[]{:S(2)}) collective-permute-start(bf16[32,3072]{1,0:T(8,128)(2,1)} %get-tuple-element.12), channel_id=1, source_target_pairs={{1,0},{2,1},{3,2},{4,3},{5,4},{6,5},{7,6},{8,7},{9,8},{10,9},{11,1... | collective-permute-start | bytes 589832 | tf_op jit(solution)/shard_map/ppermute | solution.py:493
  134.2 13.8 %collective-permute-start.2 = (bf16[32,3072]{1,0:T(8,128)(2,1)}, bf16[32,3072]{1,0:T(8,128)(2,1)}, u32[]{:S(2)}, u32[]{:S(2)}) collective-permute-start(bf16[32,3072]{1,0:T(8,128)(2,1)} %get-tuple-element.13), channel_id=1, source_target_pairs={{15,0},{0,1},{1,2},{2,3},{3,4},{4,5},{5,6},{6,7},{7,8},{8,9},{9,10... | collective-permute-start | bytes 589832 | tf_op jit(solution)/shard_map/ppermute | solution.py:493
  134.9 13.0 %collective-permute-start.3 = (bf16[32,3072]{1,0:T(8,128)(2,1)}, bf16[32,3072]{1,0:T(8,128)(2,1)}, u32[]{:S(2)}, u32[]{:S(2)}) collective-permute-start(bf16[32,3072]{1,0:T(8,128)(2,1)} %get-tuple-element.14), channel_id=1, source_target_pairs={{14,0},{15,1},{0,2},{1,3},{2,4},{3,5},{4,6},{5,7},{6,8},{7,9},{8,1... | collective-permute-start | bytes 589832 | tf_op jit(solution)/shard_map/ppermute | solution.py:493

commit v4 on v3

--- a/solution.py
+++ b/solution.py
@@ -116,46 +116,64 @@
 GROUPS = YPD * HALF
 
 
-def y_inverse_kernel(v_ref, table_ref, out_ref, rt_ref, scr_ref):
-    for lo in range(HALF):
-        for hi in range(2):
-            real = v_ref[0, 0, hi * HALF + lo].astype(BF16)
-            imag = v_ref[0, 1, hi * HALF + lo].astype(BF16)
-            base = (lo * 2 + hi) * 2 * LKX
-            rt_ref[base : base + LKX, :NY] = real
-            rt_ref[base : base + LKX, NY:] = -imag
-            rt_ref[base + LKX : base + 2 * LKX, :NY] = imag
-            rt_ref[base + LKX : base + 2 * LKX, NY:] = real
-    for pair in range(HALF // 2):
-        res = dot(table_ref[...], rt_ref[pair * 256 : (pair + 1) * 256, :], ((1,), (1,)))
-        for y in range(YPD):
-            for h in range(2):
-                start = y * HALF + pair * 2 + h
-                scr_ref[pl.ds(start, DEV, stride=GROUPS), :] = res[
-                    y * DEV : (y + 1) * DEV, h * 128 : (h + 1) * 128
-                ]
-
-    def pack(d, carry):
-        rows = scr_ref[pl.ds(pl.multiple_of(d * 8 * GROUPS, 8), 8 * GROUPS), :]
-        out_ref[pl.ds(d * 8, 8)] = rows.astype(BF16).reshape(8, GROUPS, 128)
-        return carry
-
-    lax.fori_loop(0, DEV // 8, pack, 0)
+def y_inverse_kernel(v_hbm, t_hbm, out_hbm, v_ref, t_ref, rt_ref, scr_ref, o_ref, sems):
+    loads = [pltpu.make_async_copy(v_hbm.at[c], v_ref.at[c], sems.at[c]) for c in range(3)]
+    load_table = pltpu.make_async_copy(t_hbm, t_ref, sems.at[3])
+    loads[0].start()
+    load_table.start()
+    loads[1].start()
+    loads[2].start()
+    stores = []
+    for c in range(3):
+        rt = rt_ref.at[c % 2]
+        scr = scr_ref.at[c % 2]
+        loads[c].wait()
+        for lo in range(HALF):
+            for hi in range(2):
+                real = v_ref[c, 0, hi * HALF + lo].astype(BF16)
+                imag = v_ref[c, 1, hi * HALF + lo].astype(BF16)
+                base = (lo * 2 + hi) * 2 * LKX
+                rt[base : base + LKX, :NY] = real
+                rt[base : base + LKX, NY:] = -imag
+                rt[base + LKX : base + 2 * LKX, :NY] = imag
+                rt[base + LKX : base + 2 * LKX, NY:] = real
+        if c == 0:
+            load_table.wait()
+        for quad in range(2):
+            res = dot(t_ref[...], rt[quad * 512 : (quad + 1) * 512, :], ((1,), (1,)))
+            for y in range(YPD):
+                for h in range(4):
+                    start = y * HALF + quad * 4 + h
+                    scr[pl.ds(start, DEV, stride=GROUPS), :] = res[
+                        y * DEV : (y + 1) * DEV, h * 128 : (h + 1) * 128
+                    ]
+
+        def pack(d, carry, c=c, scr=scr):
+            rows = scr[pl.ds(pl.multiple_of(d * 16 * GROUPS, 8), 16 * GROUPS), :]
+            o_ref[c, pl.ds(d * 16, 16)] = rows.astype(BF16).reshape(16, GROUPS, 128)
+            return carry
+
+        lax.fori_loop(0, DEV // 16, pack, 0)
+        here = pl.ds(c * GROUPS, GROUPS)
+        stores.append(pltpu.make_async_copy(o_ref.at[c], out_hbm.at[:, here], sems.at[4 + c]))
+        stores[-1].start()
+    for store in stores:
+        store.wait()
 
 
 def y_inverse(velocity):
     return pl.pallas_call(
         y_inverse_kernel,
-        grid=(3,),
-        in_specs=[
-            pl.BlockSpec((1, 2, LKZ, LKX, NY), lambda c: (c, 0, 0, 0, 0)),
-            pl.BlockSpec((MY, 2 * NY), lambda c: (0, 0)),
-        ],
-        out_specs=pl.BlockSpec((DEV, GROUPS, 128), lambda c: (0, c, 0)),
+        in_specs=[pl.BlockSpec(memory_space=pltpu.HBM)] * 2,
+        out_specs=pl.BlockSpec(memory_space=pltpu.HBM),
         out_shape=pltpu.HBM((DEV, MSG_IN, 128), BF16),
         scratch_shapes=[
-            pltpu.VMEM((LKZ * 2 * LKX, 2 * NY), BF16),
-            pltpu.VMEM((DEV * GROUPS, 128), F32),
+            pltpu.VMEM((3, 2, LKZ, LKX, NY), F32),
+            pltpu.VMEM((MY, 2 * NY), BF16),
+            pltpu.VMEM((2, LKZ * 2 * LKX, 2 * NY), BF16),
+            pltpu.VMEM((2, DEV * GROUPS, 128), F32),
+            pltpu.VMEM((3, DEV, GROUPS, 128), BF16),
+            pltpu.SemaphoreType.DMA((7,)),
         ],
         compiler_params=pltpu.CompilerParams(vmem_limit_bytes=60 * 2**20),
         name="y_inverse",
@@ -372,6 +390,11 @@
     )(scalars, velocity.reshape(FIELD), register.reshape(FIELD))
 
 
+def one_hot(slot_ref):
+    slots = lax.broadcasted_iota(jnp.int32, (4 * SHIFT_CAP, NY), 0)
+    return jnp.where(slots == slot_ref[...], 1.0, 0.0).astype(BF16)
+
+
 def update_kernel(
     scal_ref, g_hbm, table_ref, lin_ref, place_ref, stay_ref, base_ref, p0, p1, p2, p3, scr_ref,
     g_ref, sems,
@@ -397,6 +420,7 @@
             lax.fori_loop(part * share, (part + 1) * share, unpack, 0)
 
     table = table_ref[...]
+    place = one_hot(place_ref)
     stay = stay_ref[...]
     weight = UPDATE_WEIGHT * TIME_STEP * FORWARD_SCALE * INVERSE_SCALE * INVERSE_SCALE
     for u in range(UPDATE_PER):
@@ -432,7 +456,7 @@
                     updated = lin_ref[0, m, half, hi, u] + sign * (stress[m] - wave * pressure)
                     base_ref[m, half, hi, u] = updated * stay
                     moving.append(updated.astype(BF16))
-        packed = dot(place_ref[...], jnp.concatenate(moving, axis=0), ((1,), (1,))).astype(BF16)
+        packed = dot(place, jnp.concatenate(moving, axis=0), ((1,), (1,))).astype(BF16)
         for position, ref in enumerate((p0, p1, p2, p3)):
             ref[:, u * PACK : (u + 1) * PACK] = packed[position * SHIFT_CAP : (position + 1) * SHIFT_CAP]
 
@@ -446,7 +470,7 @@
             pl.BlockSpec(memory_space=pl.ANY),
             pl.BlockSpec((MY, 2 * NY), lambda lo: (0, 0)),
             slab_block(UPDATE_PER),
-            pl.BlockSpec((4 * SHIFT_CAP, NY), lambda lo: (0, 0)),
+            pl.BlockSpec((1, NY), lambda lo: (0, 0)),
             pl.BlockSpec((1, NY), lambda lo: (0, 0)),
         ],
         out_specs=[field_block(UPDATE_PER)] + [move_block(UPDATE_PER)] * 4,
@@ -464,7 +488,7 @@
 
 def settle_kernel(scal_ref, base_ref, a0, a1, a2, a3, place_ref, out_ref):
     arrived = jnp.concatenate([a0[...], a1[...], a2[...], a3[...]], axis=0)
-    moved = dot(arrived, place_ref[...], ((0,), (0,)))
+    moved = dot(arrived, one_hot(place_ref), ((0,), (0,)))
     keep = scal_ref[2]
     for u, hi in ((u, hi) for u in range(SETTLE_PER) for hi in range(2)):
         for m in range(3):
@@ -481,7 +505,7 @@
         grid=(HALF // SETTLE_PER,),
         in_specs=[pl.BlockSpec(memory_space=pltpu.SMEM), field_block(SETTLE_PER)]
         + [move_block(SETTLE_PER)] * 4
-        + [pl.BlockSpec((4 * SHIFT_CAP, NY), lambda lo: (0, 0))],
+        + [pl.BlockSpec((1, NY), lambda lo: (0, 0))],
         out_specs=field_block(SETTLE_PER),
         out_shape=jax.ShapeDtypeStruct(FIELD, F32),
         compiler_params=pltpu.CompilerParams(vmem_limit_bytes=16 * 2**20),
@@ -501,9 +525,11 @@
     order = jnp.arange(NY, dtype=jnp.int32)
     upto = (order[:, None] <= order[None, :]).astype(BF16)
     ranked = jnp.dot(marked.astype(BF16), upto, preferred_element_type=F32).astype(jnp.int32) - 1
-    slots = jnp.arange(SHIFT_CAP, dtype=jnp.int32)
-    place = (marked[:, None, :] & (ranked[:, None, :] == slots[None, :, None])).astype(BF16)
-    place = place.reshape(4 * SHIFT_CAP, NY)
+    slots = ranked + SHIFT_CAP * jnp.arange(4, dtype=jnp.int32)[:, None]
+    sources = col_index - jnp.array(OFFSET_VALUES, dtype=jnp.int32)[:, None]
+    inside = (sources >= 0) & (sources < COLS)
+    place = jnp.max(jnp.where(marked, slots, -1), axis=0, keepdims=True)
+    taking = jnp.max(jnp.where(marked & inside, slots, -1), axis=0, keepdims=True)
     stay = (moved_by == 0).astype(F32).reshape(1, NY)
     keep_here = jnp.sum(
         jnp.where(jnp.arange(COLS, dtype=jnp.int32) == col_index, keep_blocks, 0)
@@ -526,9 +552,6 @@
     arrivals = [
         from_behind(block, "col", value) for block, value in zip(packed, OFFSET_VALUES)
     ]
-    sources = [col_index - value for value in OFFSET_VALUES]
-    inside = jnp.stack([(source >= 0) & (source < COLS) for source in sources])
-    taking = jnp.repeat(inside, SHIFT_CAP)[:, None].astype(BF16) * place
     result = settle(scalars, base, arrivals, taking)
     return result.reshape(velocity.shape)
 

time: 153 us -> 150 us (0.980)
  waiting for transfers between devices: 81.2 us -> 84.1 us
  local copies, waits for them, and re-layouts: 3.95 us -> 1.61 us
  Pallas kernels: 40 us -> 38.3 us
  other arithmetic: 2.87 us -> 1.25 us
    ppermute x4, waiting for transfers between devices: 8.39 us -> 10.4 us  [from_behind(): lax.ppermute(block, axis, [((i - distance) % COLS, i) for i in range(COLS)])]
  transfers between devices with their start and end apart: 6 -> 6, of which waited for: 3 -> 3; matrix products, arithmetic and copies ran while one was open for 3% -> 1% of each run, Pallas kernels for 3% -> 3%
where the time goes in v4:
time: 150 us; the launch traced here: 148 us
  waiting for transfers between devices  84.1 us (56%)
  Pallas kernels  38.3 us (26%)
  starting transfers between devices  22.1 us (15%)
  local copies, waits for them, and re-layouts  1.61 us (1%)
    all_to_all x1, waiting for transfers between devices, local(): lax.all_to_all(returning, ('row', 'col'), split_axis=0, concat_axis=0, ti...  43.3 us
    all_to_all x1, waiting for transfers between devices, local(): lax.all_to_all(outgoing, ('row', 'col'), split_axis=0, concat_axis=0, til...  30.3 us
    pallas_call x1, Pallas kernels, middle(): pl.pallas_call(middle_kernel, grid=(YPD,), in_specs=[pl.BlockSpec((DEV, M...  15.1 us
    pallas_call x1, Pallas kernels, update(): pl.pallas_call(update_kernel, grid=(HALF // UPDATE_PER,), in_specs=[pl.Bl...  11.1 us
    all_to_all x1, starting transfers between devices, local(): lax.all_to_all(outgoing, ('row', 'col'), split_axis=0, concat_axis=0, til...  10.5 us
    ppermute x4, waiting for transfers between devices, from_behind(): lax.ppermute(block, axis, [((i - distance) % COLS, i) for i in range(COLS)])  10.4 us
    all_to_all x1, starting transfers between devices, local(): lax.all_to_all(returning, ('row', 'col'), split_axis=0, concat_axis=0, ti...  6.05 us
    ppermute x4, starting transfers between devices, from_behind(): lax.ppermute(block, axis, [((i - distance) % COLS, i) for i in range(COLS)])  5.62 us
  transfers between devices with their start and end apart: 6, of which 3 were waited for; matrix products, arithmetic and copies ran while one was open for 1% of the time, Pallas kernels for 3%

profile of v4, /device:TPU:8, one launch (start us, length us, event | category | flops | bytes accessed | tf_op | source)
XLA Modules:
  0.0 148.4 jit_solution(11434137951174867725)
XLA Ops:
  0.0 4.6 %y_inverse.1 = bf16[128,72,128]{2,1,0:T(8,128)(2,1)} custom-call(f32[3,2,16,32,256]{4,3,2,1,0:T(8,128)} %v_hbm.1, bf16[384,512]{1,0:T(8,128)(2,1)} %constant.54.clone.t_hbm.table_ref), custom_call_target="tpu_custom_call" | custom-call | tf_op jit(solution)/shard_map/y_inverse/pallas_call | solution.py:165
  4.6 0.0 copy-start.4
  4.6 0.0 copy-start.6
  4.6 0.0 copy-start.1
  4.6 0.0 copy-start.3
  4.6 10.5 %all-to-all-start = ((bf16[128,72,128]{2,1,0:T(8,128)(2,1)}), bf16[128,72,128]{2,1,0:T(8,128)(2,1)S(1)}, u32[]{:S(2)}, u32[]{:S(2)}) async-start(bf16[128,72,128]{2,1,0:T(8,128)(2,1)} %y_inverse.1), calls=%async_computation | async-start | bytes 4718592 | tf_op jit(solution)/shard_map/all_to_all | solution.py:547
  15.1 0.8 copy-done.5
  15.9 0.7 copy-done.7
  16.7 0.2 x_table.1.x_ref
  16.9 30.3 %all-to-all-done.m_ref = bf16[128,72,128]{2,1,0:T(8,128)(2,1)S(1)} async-done(((bf16[128,72,128]{2,1,0:T(8,128)(2,1)}), bf16[128,72,128]{2,1,0:T(8,128)(2,1)S(1)}, u32[]{:S(2)}, u32[]{:S(2)}) %all-to-all-start) | async-done | bytes 2359328 | tf_op jit(solution)/shard_map/all_to_all | solution.py:547
  47.2 15.1 %middle.1 = bf16[128,120,128]{2,1,0:T(8,128)(2,1)} custom-call(bf16[128,72,128]{2,1,0:T(8,128)(2,1)S(1)} %all-to-all-done.m_ref, bf16[512,768]{1,0:T(8,128)(2,1)S(1)} %x_table.1.x_ref, bf16[384,256]{1,0:T(8,128)(2,1)S(1)} %copy-done.1, bf16[128,208]{1,0:T(8,128)(2,1)S(1)} %copy-done.3, bf16[128,192]{1,0:T(8,128)(2,1)S(1)} %copy-done.2), custom_call_target="tpu_custom_call" | custom-call | tf_op jit(solution)/shard_map/middle/pallas_call | solution.py:308
  62.3 6.1 %all-to-all-start.1 = ((bf16[128,120,128]{2,1,0:T(8,128)(2,1)}), bf16[128,120,128]{2,1,0:T(8,128)(2,1)}, u32[]{:S(2)}, u32[]{:S(2)}) async-start(bf16[128,120,128]{2,1,0:T(8,128)(2,1)} %middle.1), calls=%async_computation.1 | async-start | bytes 7864320 | tf_op jit(solution)/shard_map/all_to_all | solution.py:549
  68.3 0.6 fusion.2
  69.7 0.6 pad_maximum_fusion.scal_ref
  70.3 4.7 %linear.1.lin_ref = f32[8,3,2,2,8,32,256]{6,5,4,3,2,1,0:T(8,128)} custom-call(f32[3]{0:T(128)} %pad_maximum_fusion.scal_ref, f32[3,2,2,8,32,256]{5,4,3,2,1,0:T(8,128)} %bitcast.12, f32[3,2,2,8,32,256]{5,4,3,2,1,0:T(8,128)} %bitcast.13), custom_call_target="tpu_custom_call" | custom-call | tf_op jit(solution)/shard_map/linear/pallas_call | solution.py:382
  75.0 0.2 select_reduce_fusion
  75.2 43.3 %all-to-all-done.1.g_hbm = bf16[128,120,128]{2,1,0:T(8,128)(2,1)} async-done(((bf16[128,120,128]{2,1,0:T(8,128)(2,1)}), bf16[128,120,128]{2,1,0:T(8,128)(2,1)}, u32[]{:S(2)}, u32[]{:S(2)}) %all-to-all-start.1) | async-done | bytes 3932192 | tf_op jit(solution)/shard_map/all_to_all | solution.py:549
  118.5 11.1 %update.1 = (f32[3,2,2,8,32,256]{5,4,3,2,1,0:T(8,128)S(1)}, bf16[32,3072]{1,0:T(8,128)(2,1)S(1)}, bf16[32,3072]{1,0:T(8,128)(2,1)S(1)}, bf16[32,3072]{1,0:T(8,128)(2,1)S(1)}, bf16[32,3072]{1,0:T(8,128)(2,1)S(1)}) custom-call(f32[3]{0:T(128)S(1)} %copy-done.8, bf16[128,120,128]{2,1,0:T(8,128)(2,1)} %all-to-all-done.1.g_hbm, bf16[384,512]{1,0:T(8,128)(2,1)S(1)} %copy-done, ...), custom_call_target="tpu_custom_call" | custom-call | tf_op jit(solution)/shard_map/update/pallas_call | solution.py:465
  129.6 0.1 collective-permute-start
  129.7 2.4 %collective-permute-start.1 = (bf16[32,3072]{1,0:T(8,128)(2,1)S(1)}, bf16[32,3072]{1,0:T(8,128)(2,1)S(1)}, u32[]{:S(2)}, u32[]{:S(2)}) collective-permute-start(bf16[32,3072]{1,0:T(8,128)(2,1)S(1)} %get-tuple-element.12), channel_id=1, source_target_pairs={{1,0},{2,1},{3,2},{4,3},{5,4},{6,5},{7,6},{8,7},{9,8},{10,9},{11,1... | collective-permute-start | bytes 589832 | tf_op jit(solution)/shard_map/ppermute | solution.py:517
  132.1 0.8 collective-permute-start.2
  132.9 2.4 %collective-permute-start.3 = (bf16[32,3072]{1,0:T(8,128)(2,1)S(1)}, bf16[32,3072]{1,0:T(8,128)(2,1)S(1)}, u32[]{:S(2)}, u32[]{:S(2)}) collective-permute-start(bf16[32,3072]{1,0:T(8,128)(2,1)S(1)} %get-tuple-element.14), channel_id=1, source_target_pairs={{14,0},{15,1},{0,2},{1,3},{2,4},{3,5},{4,6},{5,7},{6,8},{7,9},{8,1... | collective-permute-start | bytes 589832 | tf_op jit(solution)/shard_map/ppermute | solution.py:517
  135.2 10.4 %collective-permute-done.a0 = bf16[32,3072]{1,0:T(8,128)(2,1)S(1)} collective-permute-done((bf16[32,3072]{1,0:T(8,128)(2,1)S(1)}, bf16[32,3072]{1,0:T(8,128)(2,1)S(1)}, u32[]{:S(2)}, u32[]{:S(2)}) %collective-permute-start) | collective-permute-done | bytes 196640 | tf_op jit(solution)/shard_map/ppermute | solution.py:517
  145.7 2.8 %settle.1 = f32[3,2,2,8,32,256]{5,4,3,2,1,0:T(8,128)} custom-call(f32[3]{0:T(128)S(1)} %copy-done.8, f32[3,2,2,8,32,256]{5,4,3,2,1,0:T(8,128)S(1)} %get-tuple-element.10.base_ref, bf16[32,3072]{1,0:T(8,128)(2,1)S(1)} %collective-permute-done.a0, bf16[32,3072]{1,0:T(8,128)(2,1)S(1)} %collective-permute-done.1.a1, ...), custom_call_target="tpu_custom_call" | custom-call | tf_op jit(solution)/shard_map/settle/pallas_call | solution.py:503
  (31 shorter events, 0.1 us)
Async XLA Ops:
  4.6 10.5 %copy-start.4 = (f32[32,384]{1,0:T(8,128)S(1)}, f32[32,384]{1,0:T(8,128)}, u32[]{:S(2)}) copy-start(f32[32,384]{1,0:T(8,128)} %constant.58.clone.fine_sin) | copy-start | bytes 147460
  4.6 10.5 %copy-start.6 = (f32[16,384]{1,0:T(8,128)S(1)}, f32[16,384]{1,0:T(8,128)}, u32[]{:S(2)}) copy-start(f32[16,384]{1,0:T(8,128)} %constant.56.clone.coarse_sin) | copy-start | bytes 73732
  4.6 42.6 %copy-start.1 = (bf16[384,256]{1,0:T(8,128)(2,1)S(1)}, bf16[384,256]{1,0:T(8,128)(2,1)}, u32[]{:S(2)}) copy-start(bf16[384,256]{1,0:T(8,128)(2,1)} %constant.59.clone.zi_ref) | copy-start | bytes 589828
  4.6 42.6 %copy-start.2 = (bf16[128,192]{1,0:T(8,128)(2,1)S(1)}, bf16[128,192]{1,0:T(8,128)(2,1)}, u32[]{:S(2)}) copy-start(bf16[128,192]{1,0:T(8,128)(2,1)} %constant.61.clone.zm_ref) | copy-start | bytes 147460
  4.6 42.6 %copy-start.3 = (bf16[128,208]{1,0:T(8,128)(2,1)S(1)}, bf16[128,208]{1,0:T(8,128)(2,1)}, u32[]{:S(2)}) copy-start(bf16[128,208]{1,0:T(8,128)(2,1)} %constant.60.clone.zr_ref) | copy-start | bytes 159748
  4.6 42.6 %all-to-all-start = ((bf16[128,72,128]{2,1,0:T(8,128)(2,1)}), bf16[128,72,128]{2,1,0:T(8,128)(2,1)S(1)}, u32[]{:S(2)}, u32[]{:S(2)}) async-start(bf16[128,72,128]{2,1,0:T(8,128)(2,1)} %y_inverse.1), calls=%async_computation | async-start | bytes 4718592 | tf_op jit(solution)/shard_map/all_to_all | solution.py:547
  15.1 0.8 copy-start.5
  15.9 0.7 copy-start.7
  62.3 6.1 %copy-start.11 = (s32[16]{0:T(128)S(1)}, s32[16]{0:T(128)}, u32[]{:S(2)}) copy-start(s32[16]{0:T(128)} %param.19) | copy-start | bytes 196
  62.3 7.4 %copy-start.9 = (s32[256]{0:T(256)S(1)}, s32[256]{0:T(256)}, u32[]{:S(2)}) copy-start(s32[256]{0:T(256)} %param.17) | copy-start | bytes 3076
  62.3 7.4 %copy-start.10 = (s32[256]{0:T(256)S(1)}, s32[256]{0:T(256)}, u32[]{:S(2)}) copy-start(s32[256]{0:T(256)} %param.18) | copy-start | bytes 3076
  62.3 56.3 %all-to-all-start.1 = ((bf16[128,120,128]{2,1,0:T(8,128)(2,1)}), bf16[128,120,128]{2,1,0:T(8,128)(2,1)}, u32[]{:S(2)}, u32[]{:S(2)}) async-start(bf16[128,120,128]{2,1,0:T(8,128)(2,1)} %middle.1), calls=%async_computation.1 | async-start | bytes 7864320 | tf_op jit(solution)/shard_map/all_to_all | solution.py:549
  70.3 4.7 %copy-start.12 = (s32[4]{0:T(128)S(1)}, s32[4]{0:T(128)}, u32[]{:S(2)}) copy-start(s32[4]{0:T(128)} %constant.62) | copy-start | bytes 52
  70.3 48.2 %copy-start = (bf16[384,512]{1,0:T(8,128)(2,1)S(1)}, bf16[384,512]{1,0:T(8,128)(2,1)}, u32[]{:S(2)}) copy-start(bf16[384,512]{1,0:T(8,128)(2,1)} %constant.54.clone.t_hbm.table_ref) | copy-start | bytes 1179652
  70.3 48.2 %copy-start.8 = (f32[3]{0:T(128)S(1)}, f32[3]{0:T(128)}, u32[]{:S(2)}) copy-start(f32[3]{0:T(128)} %pad_maximum_fusion.scal_ref) | copy-start | bytes 40
  129.6 16.1 %collective-permute-start = (bf16[32,3072]{1,0:T(8,128)(2,1)S(1)}, bf16[32,3072]{1,0:T(8,128)(2,1)S(1)}, u32[]{:S(2)}, u32[]{:S(2)}) collective-permute-start(bf16[32,3072]{1,0:T(8,128)(2,1)S(1)} %get-tuple-element.11), channel_id=1, source_target_pairs={{2,0},{3,1},{4,2},{5,3},{6,4},{7,5},{8,6},{9,7},{10,8},{11,9},{12,... | collective-permute-start | bytes 589832 | tf_op jit(solution)/shard_map/ppermute | solution.py:517
  129.7 16.0 %collective-permute-start.1 = (bf16[32,3072]{1,0:T(8,128)(2,1)S(1)}, bf16[32,3072]{1,0:T(8,128)(2,1)S(1)}, u32[]{:S(2)}, u32[]{:S(2)}) collective-permute-start(bf16[32,3072]{1,0:T(8,128)(2,1)S(1)} %get-tuple-element.12), channel_id=1, source_target_pairs={{1,0},{2,1},{3,2},{4,3},{5,4},{6,5},{7,6},{8,7},{9,8},{10,9},{11,1... | collective-permute-start | bytes 589832 | tf_op jit(solution)/shard_map/ppermute | solution.py:517
  132.1 13.6 %collective-permute-start.2 = (bf16[32,3072]{1,0:T(8,128)(2,1)S(1)}, bf16[32,3072]{1,0:T(8,128)(2,1)S(1)}, u32[]{:S(2)}, u32[]{:S(2)}) collective-permute-start(bf16[32,3072]{1,0:T(8,128)(2,1)S(1)} %get-tuple-element.13), channel_id=1, source_target_pairs={{15,0},{0,1},{1,2},{2,3},{3,4},{4,5},{5,6},{6,7},{7,8},{8,9},{9,10... | collective-permute-start | bytes 589832 | tf_op jit(solution)/shard_map/ppermute | solution.py:517
  132.9 12.8 %collective-permute-start.3 = (bf16[32,3072]{1,0:T(8,128)(2,1)S(1)}, bf16[32,3072]{1,0:T(8,128)(2,1)S(1)}, u32[]{:S(2)}, u32[]{:S(2)}) collective-permute-start(bf16[32,3072]{1,0:T(8,128)(2,1)S(1)} %get-tuple-element.14), channel_id=1, source_target_pairs={{14,0},{15,1},{0,2},{1,3},{2,4},{3,5},{4,6},{5,7},{6,8},{7,9},{8,1... | collective-permute-start | bytes 589832 | tf_op jit(solution)/shard_map/ppermute | solution.py:517
